TPU v7x, 128 devices: a whole 4x4x4 slice. The times are simulated.
128 devices in a mesh: rows: 128 (over x, z, y, core).
Axes of the slice: x: 4, y: 4, z: 4, core: 2. Of those that a mesh axis runs over, the one named last changes fastest.
Arguments:
- tile_values: float32 [26624, 128, 128], P('rows'), as said below
- tile_row: int32 [26624], P('rows'), may hold values from 0 to 15, as said below
- tile_slot: int32 [26624], P('rows'), may hold values from 0 to 143, as said below
- tile_count: int32 [128], P('rows'), may hold values from 144 to 208, as said below
- requests: int32 [128, 128, 1], P('rows'), may hold values from 0 to 15
- right_side: float32 [2048, 4, 128], P('rows')
Outputs:
- solution: float32 [2048, 4, 128], P('rows')
- hessenberg: float32 [4, 4, 3], replicated
Inputs may be any that keep to these rules, and one draw needn't show every extreme that they name: `tile_row`: tile t < 16 of every device lies in block row t; it is the diagonal tile of that row. `tile_slot`: slot s < 16 is the device's own block s; slot 16 + o + q is the q-th block requested from device o; tile t < 144 of every device uses slot t. `tile_count`: some device uses all 208 slots. requests[d, o, q] is a block index among device o's 16 block rows. `tile_values`: tile t < 16 of every device holds the diagonal block of its row.
All inputs are finite; a program needn't handle non-finite values.
Results may differ from a plain program's by a relative error of at most 0.0003.
Values sent between devices are 32-bit elements; how exact they have to be, the bound alone decides.
No kernel may reach another device: no remote copies, remote signals or barrier semaphores. Data moves between devices by JAX's collectives and lax.ppermute only.
A program may use at most 64 MiB of HBM per device.

v0:
```python
import functools

import jax
import jax.numpy as jnp
from jax import lax
from jax.sharding import Mesh
from jax.sharding import PartitionSpec as P

ITERS = 3
ROWS = ("rows_0", "rows_1", "rows_2", "rows_3")


epsilon = 1e-06
highest = lax.Precision.HIGHEST


def by_axis(shard, axes):
    return functools.reduce(lax.psum, axes, shard)


def least_squares(hessenberg, beta_norm):
    krylov = hessenberg.shape[2]
    triangle = hessenberg
    target = jnp.zeros((hessenberg.shape[0], krylov + 1), jnp.float32).at[:, 0].set(beta_norm)
    cosines = []
    sine_list = []
    for column in range(krylov):
        column_vals = triangle[:, :, column]
        for earlier in range(column):
            first_entry = column_vals[:, earlier]
            second = column_vals[:, earlier + 1]
            column_vals = column_vals.at[:, earlier].set(
                cosines[earlier] * first_entry + sine_list[earlier] * second
            )
            column_vals = column_vals.at[:, earlier + 1].set(
                cosines[earlier] * second - sine_list[earlier] * first_entry
            )
        first_entry = column_vals[:, column]
        second = column_vals[:, column + 1]
        radius = jnp.sqrt(first_entry * first_entry + second * second)
        cosine = first_entry / radius
        sine_term = second / radius
        cosines.append(cosine)
        sine_list.append(sine_term)
        column_vals = column_vals.at[:, column].set(radius).at[:, column + 1].set(0.0)
        triangle = triangle.at[:, :, column].set(column_vals)
        leading = target[:, column]
        target = (
            target.at[:, column].set(cosine * leading).at[:, column + 1].set(-sine_term * leading)
        )
    weights = jnp.zeros((hessenberg.shape[0], krylov), jnp.float32)
    for column in reversed(range(krylov)):
        partial_sum = target[:, column] - jnp.sum(
            triangle[:, column, column + 1 : krylov] * weights[:, column + 1 :], axis=1
        )
        weights = weights.at[:, column].set(partial_sum / triangle[:, column, column])
    return weights


def local_squares(vector):
    return jnp.sum(vector * vector, axis=(0, 2))


def on_device(tile_values, tile_row, tile_slot, tile_count, requests, right_side):
    tile_total = tile_values.shape[0]
    row_blocks = right_side.shape[0]
    devices = lax.axis_size(ROWS)
    position = jnp.arange(tile_total, dtype=jnp.int32)
    live_mask = (position < tile_count[0]).astype(jnp.float32)
    block_ids = jnp.arange(row_blocks, dtype=jnp.int32)
    row_onehot = (tile_row[None, :] == block_ids[:, None]).astype(jnp.float32) * live_mask[None, :]
    own_requests = requests[0]
    asked_blocks = lax.all_to_all(
        own_requests, ROWS, split_axis=0, concat_axis=0, tiled=True
    ).reshape(-1)
    beta_norm = jnp.sqrt(by_axis(local_squares(right_side), ROWS) + epsilon)
    basis_list = [right_side / beta_norm[None, :, None]]
    hessenberg = jnp.zeros((right_side.shape[1], ITERS + 1, ITERS), jnp.float32)
    for column in range(ITERS):
        vector = basis_list[column]
        outgoing = vector[asked_blocks].reshape(devices, -1, vector.shape[1], vector.shape[2])
        incoming = lax.all_to_all(outgoing, ROWS, split_axis=0, concat_axis=0, tiled=True)
        slot_table = jnp.concatenate(
            [vector, incoming.reshape(-1, vector.shape[1], vector.shape[2])], axis=0
        )
        picked = slot_table[tile_slot]
        products = jnp.einsum("tij,tkj->tki", tile_values, picked, precision=highest)
        candidate = jnp.einsum("rt,tki->rki", row_onehot, products, precision=highest)
        stacked = jnp.stack(basis_list)
        local_terms = jnp.concatenate(
            [
                jnp.einsum("jrki,rki->jk", stacked, candidate, precision=highest),
                local_squares(candidate)[None, :],
            ],
            axis=0,
        )
        summed = by_axis(local_terms, ROWS)
        coefficients = summed[: column + 1]
        candidate = candidate - jnp.einsum("jk,jrki->rki", coefficients, stacked, precision=highest)
        hessenberg = hessenberg.at[:, : column + 1, column].set(jnp.transpose(coefficients))
        remainder = summed[column + 1] - jnp.sum(coefficients * coefficients, axis=0)
        length = jnp.sqrt(jnp.maximum(remainder, 0.0) + epsilon)
        hessenberg = hessenberg.at[:, column + 1, column].set(length)
        if column + 1 < ITERS:
            basis_list.append(candidate / length[None, :, None])
    weights = least_squares(hessenberg, beta_norm)
    solution = jnp.einsum("kj,jrki->rki", weights, jnp.stack(basis_list), precision=highest)
    return (solution, hessenberg)


def solution(mesh):
    finer = Mesh(mesh.devices.reshape(4, 4, 4, 2), ("rows_0", "rows_1", "rows_2", "rows_3"))
    placed = (
        P(ROWS, None, None),
        P(ROWS),
        P(ROWS),
        P(ROWS),
        P(ROWS, None, None),
        P(ROWS, None, None),
    )
    return jax.shard_map(
        on_device,
        mesh=finer,
        in_specs=placed,
        out_specs=(P(ROWS, None, None), P()),
        check_vma=False,
    )
```

profile of v0, /device:TPU:1, one launch (start us, length us, event | category | flops | bytes accessed | tf_op | source)
XLA Modules:
  0.0 291.7 jit_solution(4035739901747230183)
XLA Ops:
  1.6 9.3 %psum.112 = f32[4]{0:T(128)S(1)} all-reduce(f32[4]{0:T(128)S(1)} %multiply_reduce_fusion.4), channel_id=1, replica_groups=mesh['rows_0'=4,'rows_1'=4,'rows_2'=4,'rows_3'=2] {'rows_0'}, use_global_device_ids=true, to_apply=%region_1.0 | all-reduce | flops 4 | bytes 32 | tf_op jit(solution)/shard_map/psum | solution.py:18
  10.9 9.7 %psum.113 = f32[4]{0:T(128)S(1)} all-reduce(f32[4]{0:T(128)S(1)} %psum.112), channel_id=1, replica_groups=mesh['rows_0'=4,'rows_1'=4,'rows_2'=4,'rows_3'=2] {'rows_1'}, use_global_device_ids=true, to_apply=%region_2.0 | all-reduce | flops 4 | bytes 32 | tf_op jit(solution)/shard_map/psum | solution.py:18
  20.6 8.7 %psum.114 = f32[4]{0:T(128)S(1)} all-reduce(f32[4]{0:T(128)S(1)} %psum.113), channel_id=1, replica_groups=mesh['rows_0'=4,'rows_1'=4,'rows_2'=4,'rows_3'=2] {'rows_2'}, use_global_device_ids=true, to_apply=%region_3.0 | all-reduce | flops 4 | bytes 32 | tf_op jit(solution)/shard_map/psum | solution.py:18
  30.7 10.1 %all-to-all-start = ((s32[128,1,1]{2,1,0:T(1,128)}), s32[128,1,1]{2,1,0:T(1,128)S(1)}, u32[]{:S(2)}, u32[]{:S(2)}) async-start(s32[128,1,1]{2,1,0:T(1,128)} %copy.94), calls=%async_computation | async-start | bytes 131072 | tf_op jit(solution)/shard_map/all_to_all | solution.py:73
  40.8 3.3 %psum.115 = f32[4]{0:T(128)S(1)} all-reduce(f32[4]{0:T(128)S(1)} %psum.114), channel_id=1, replica_groups=mesh['rows_0'=4,'rows_1'=4,'rows_2'=4,'rows_3'=2] {'rows_3'}, use_global_device_ids=true, to_apply=%region_4.0 | all-reduce | flops 4 | bytes 32 | tf_op jit(solution)/shard_map/psum | solution.py:18
  45.1 5.5 %all-to-all-done = s32[128,1,1]{2,1,0:T(1,128)S(1)} async-done(((s32[128,1,1]{2,1,0:T(1,128)}), s32[128,1,1]{2,1,0:T(1,128)S(1)}, u32[]{:S(2)}, u32[]{:S(2)}) %all-to-all-start) | async-done | bytes 544 | tf_op jit(solution)/shard_map/all_to_all | solution.py:73
  50.5 2.3 reduce.93
  52.9 1.4 gather_fusion
  54.3 4.9 %all-to-all-start.1 = ((f32[128,1,4,128]{3,2,1,0:T(4,128)}), f32[128,1,4,128]{3,2,1,0:T(4,128)S(1)}, u32[]{:S(2)}, u32[]{:S(2)}) async-start(f32[128,1,4,128]{3,2,1,0:T(4,128)} %bitcast.8), calls=%async_computation.1 | async-start | bytes 524288 | tf_op jit(solution)/shard_map/all_to_all | solution.py:82
  60.6 9.4 %all-to-all-done.1 = f32[128,1,4,128]{3,2,1,0:T(4,128)S(1)} async-done(((f32[128,1,4,128]{3,2,1,0:T(4,128)}), f32[128,1,4,128]{3,2,1,0:T(4,128)S(1)}, u32[]{:S(2)}, u32[]{:S(2)}) %all-to-all-start.1) | async-done | bytes 262176 | tf_op jit(solution)/shard_map/all_to_all | solution.py:82
  70.9 24.2 %fusion.56 = f32[208,4,128]{2,1,0:T(4,128)S(1)} fusion(f32[208,4,128]{2,1,0:T(4,128)S(1)} %gather_fusion.1, f32[208,128,128]{2,1,0:T(8,128)} %param.68), kind=kOutput, calls=%fused_computation.141 | convolution fusion | flops 163577856 | bytes 14483456 | tf_op jit(solution)/shard_map/tij,tkj->tki/dot_general | solution.py:87
  95.8 6.9 %psum.116 = f32[2,4]{1,0:T(2,128)S(1)} all-reduce(f32[2,4]{1,0:T(2,128)S(1)} %pad_maximum_fusion.7), channel_id=1, replica_groups=mesh['rows_0'=4,'rows_1'=4,'rows_2'=4,'rows_3'=2] {'rows_0'}, use_global_device_ids=true, to_apply=%region_6.0 | all-reduce | flops 8 | bytes 64 | tf_op jit(solution)/shard_map/psum | solution.py:18
  102.7 6.9 %psum.117 = f32[2,4]{1,0:T(2,128)S(1)} all-reduce(f32[2,4]{1,0:T(2,128)S(1)} %psum.116), channel_id=1, replica_groups=mesh['rows_0'=4,'rows_1'=4,'rows_2'=4,'rows_3'=2] {'rows_1'}, use_global_device_ids=true, to_apply=%region_7.0 | all-reduce | flops 8 | bytes 64 | tf_op jit(solution)/shard_map/psum | solution.py:18
  109.7 6.9 %psum.118 = f32[2,4]{1,0:T(2,128)S(1)} all-reduce(f32[2,4]{1,0:T(2,128)S(1)} %psum.117), channel_id=1, replica_groups=mesh['rows_0'=4,'rows_1'=4,'rows_2'=4,'rows_3'=2] {'rows_2'}, use_global_device_ids=true, to_apply=%region_8.0 | all-reduce | flops 8 | bytes 64 | tf_op jit(solution)/shard_map/psum | solution.py:18
  116.6 8.6 %psum.119 = f32[2,4]{1,0:T(2,128)S(1)} all-reduce(f32[2,4]{1,0:T(2,128)S(1)} %psum.118), channel_id=1, replica_groups=mesh['rows_0'=4,'rows_1'=4,'rows_2'=4,'rows_3'=2] {'rows_3'}, use_global_device_ids=true, to_apply=%region_9.0 | all-reduce | flops 8 | bytes 64 | tf_op jit(solution)/shard_map/psum | solution.py:18
  125.3 1.4 gather_fusion.2
  126.7 4.1 %all-to-all-start.2 = ((f32[128,1,4,128]{3,2,1,0:T(4,128)}), f32[128,1,4,128]{3,2,1,0:T(4,128)S(1)}, u32[]{:S(2)}, u32[]{:S(2)}) async-start(f32[128,1,4,128]{3,2,1,0:T(4,128)} %bitcast.16), calls=%async_computation.2 | async-start | bytes 524288 | tf_op jit(solution)/shard_map/all_to_all | solution.py:82
  134.2 7.5 %all-to-all-done.2 = f32[128,1,4,128]{3,2,1,0:T(4,128)S(1)} async-done(((f32[128,1,4,128]{3,2,1,0:T(4,128)}), f32[128,1,4,128]{3,2,1,0:T(4,128)S(1)}, u32[]{:S(2)}, u32[]{:S(2)}) %all-to-all-start.2) | async-done | bytes 262176 | tf_op jit(solution)/shard_map/all_to_all | solution.py:82
  142.6 24.2 %fusion.57 = f32[208,4,128]{2,1,0:T(4,128)S(1)} fusion(f32[208,4,128]{2,1,0:T(4,128)S(1)} %gather_fusion.3, f32[208,128,128]{2,1,0:T(8,128)} %param.68), kind=kOutput, calls=%fused_computation.142 | convolution fusion | flops 163577856 | bytes 14483456 | tf_op jit(solution)/shard_map/tij,tkj->tki/dot_general | solution.py:87
  168.7 6.8 %psum.120 = f32[3,4]{1,0:T(4,128)S(1)} all-reduce(f32[3,4]{1,0:T(4,128)S(1)} %pad_maximum_fusion.5), channel_id=1, replica_groups=mesh['rows_0'=4,'rows_1'=4,'rows_2'=4,'rows_3'=2] {'rows_0'}, use_global_device_ids=true, to_apply=%region_11.0 | all-reduce | flops 12 | bytes 96 | tf_op jit(solution)/shard_map/psum | solution.py:18
  176.2 6.9 %psum.121 = f32[3,4]{1,0:T(4,128)S(1)} all-reduce(f32[3,4]{1,0:T(4,128)S(1)} %psum.120), channel_id=1, replica_groups=mesh['rows_0'=4,'rows_1'=4,'rows_2'=4,'rows_3'=2] {'rows_1'}, use_global_device_ids=true, to_apply=%region_12.0 | all-reduce | flops 12 | bytes 96 | tf_op jit(solution)/shard_map/psum | solution.py:18
  183.1 6.9 %psum.122 = f32[3,4]{1,0:T(4,128)S(1)} all-reduce(f32[3,4]{1,0:T(4,128)S(1)} %psum.121), channel_id=1, replica_groups=mesh['rows_0'=4,'rows_1'=4,'rows_2'=4,'rows_3'=2] {'rows_2'}, use_global_device_ids=true, to_apply=%region_13.0 | all-reduce | flops 12 | bytes 96 | tf_op jit(solution)/shard_map/psum | solution.py:18
  190.1 8.6 %psum.123 = f32[3,4]{1,0:T(4,128)S(1)} all-reduce(f32[3,4]{1,0:T(4,128)S(1)} %psum.122), channel_id=1, replica_groups=mesh['rows_0'=4,'rows_1'=4,'rows_2'=4,'rows_3'=2] {'rows_3'}, use_global_device_ids=true, to_apply=%region_14.0 | all-reduce | flops 12 | bytes 96 | tf_op jit(solution)/shard_map/psum | solution.py:18
  200.7 3.8 %all-to-all-start.3 = ((f32[128,1,4,128]{3,2,1,0:T(4,128)}), f32[128,1,4,128]{3,2,1,0:T(4,128)S(1)}, u32[]{:S(2)}, u32[]{:S(2)}) async-start(f32[128,1,4,128]{3,2,1,0:T(4,128)} %bitcast.39), calls=%async_computation.3 | async-start | bytes 524288 | tf_op jit(solution)/shard_map/all_to_all | solution.py:82
  206.1 9.3 %all-to-all-done.3 = f32[128,1,4,128]{3,2,1,0:T(4,128)S(1)} async-done(((f32[128,1,4,128]{3,2,1,0:T(4,128)}), f32[128,1,4,128]{3,2,1,0:T(4,128)S(1)}, u32[]{:S(2)}, u32[]{:S(2)}) %all-to-all-start.3) | async-done | bytes 262176 | tf_op jit(solution)/shard_map/all_to_all | solution.py:82
  216.3 24.2 %fusion.58 = f32[208,4,128]{2,1,0:T(4,128)S(1)} fusion(f32[208,4,128]{2,1,0:T(4,128)S(1)} %gather_fusion.5, f32[208,128,128]{2,1,0:T(8,128)} %param.68), kind=kOutput, calls=%fused_computation.143 | convolution fusion | flops 163577856 | bytes 14483456 | tf_op jit(solution)/shard_map/tij,tkj->tki/dot_general | solution.py:87
  241.7 6.9 %psum.124 = f32[4,4]{1,0:T(4,128)S(1)} all-reduce(f32[4,4]{1,0:T(4,128)S(1)} %pad_maximum_fusion.6), channel_id=1, replica_groups=mesh['rows_0'=4,'rows_1'=4,'rows_2'=4,'rows_3'=2] {'rows_0'}, use_global_device_ids=true, to_apply=%region_20.0 | all-reduce | flops 16 | bytes 128 | tf_op jit(solution)/shard_map/psum | solution.py:18
  248.6 6.9 %psum.125 = f32[4,4]{1,0:T(4,128)S(1)} all-reduce(f32[4,4]{1,0:T(4,128)S(1)} %psum.124), channel_id=1, replica_groups=mesh['rows_0'=4,'rows_1'=4,'rows_2'=4,'rows_3'=2] {'rows_1'}, use_global_device_ids=true, to_apply=%region_21.0 | all-reduce | flops 16 | bytes 128 | tf_op jit(solution)/shard_map/psum | solution.py:18
  255.6 6.9 %psum.126 = f32[4,4]{1,0:T(4,128)S(1)} all-reduce(f32[4,4]{1,0:T(4,128)S(1)} %psum.125), channel_id=1, replica_groups=mesh['rows_0'=4,'rows_1'=4,'rows_2'=4,'rows_3'=2] {'rows_2'}, use_global_device_ids=true, to_apply=%region_22.0 | all-reduce | flops 16 | bytes 128 | tf_op jit(solution)/shard_map/psum | solution.py:18
  262.4 8.6 %psum.127 = f32[4,4]{1,0:T(4,128)S(1)} all-reduce(f32[4,4]{1,0:T(4,128)S(1)} %psum.126), channel_id=1, replica_groups=mesh['rows_0'=4,'rows_1'=4,'rows_2'=4,'rows_3'=2] {'rows_3'}, use_global_device_ids=true, to_apply=%region_23.0 | all-reduce | flops 16 | bytes 128 | tf_op jit(solution)/shard_map/psum | solution.py:18
  271.0 1.8 broadcast_select_fusion
  286.3 2.1 fusion.35
  (127 shorter events, 34.6 us)
Async XLA Ops:
  0.6 95.0 %copy-start = (f32[16,4,128]{2,1,0:T(4,128)S(1)}, f32[16,4,128]{2,1,0:T(4,128)}, u32[]{:S(2)}) copy-start(f32[16,4,128]{2,1,0:T(4,128)} %param.73) | copy-start | bytes 98308
  0.6 94.5 %copy-start.1 = (s32[208]{0:T(256)S(1)}, s32[208]{0:T(256)}, u32[]{:S(2)}) copy-start(s32[208]{0:T(256)} %param.69) | copy-start | bytes 2500
  30.7 19.8 %all-to-all-start = ((s32[128,1,1]{2,1,0:T(1,128)}), s32[128,1,1]{2,1,0:T(1,128)S(1)}, u32[]{:S(2)}, u32[]{:S(2)}) async-start(s32[128,1,1]{2,1,0:T(1,128)} %copy.94), calls=%async_computation | async-start | bytes 131072 | tf_op jit(solution)/shard_map/all_to_all | solution.py:73
  54.3 15.6 %all-to-all-start.1 = ((f32[128,1,4,128]{3,2,1,0:T(4,128)}), f32[128,1,4,128]{3,2,1,0:T(4,128)S(1)}, u32[]{:S(2)}, u32[]{:S(2)}) async-start(f32[128,1,4,128]{3,2,1,0:T(4,128)} %bitcast.8), calls=%async_computation.1 | async-start | bytes 524288 | tf_op jit(solution)/shard_map/all_to_all | solution.py:82
  126.7 14.9 %all-to-all-start.2 = ((f32[128,1,4,128]{3,2,1,0:T(4,128)}), f32[128,1,4,128]{3,2,1,0:T(4,128)S(1)}, u32[]{:S(2)}, u32[]{:S(2)}) async-start(f32[128,1,4,128]{3,2,1,0:T(4,128)} %bitcast.16), calls=%async_computation.2 | async-start | bytes 524288 | tf_op jit(solution)/shard_map/all_to_all | solution.py:82
  200.7 14.7 %all-to-all-start.3 = ((f32[128,1,4,128]{3,2,1,0:T(4,128)}), f32[128,1,4,128]{3,2,1,0:T(4,128)S(1)}, u32[]{:S(2)}, u32[]{:S(2)}) async-start(f32[128,1,4,128]{3,2,1,0:T(4,128)} %bitcast.39), calls=%async_computation.3 | async-start | bytes 524288 | tf_op jit(solution)/shard_map/all_to_all | solution.py:82
where the time goes:
time: 296 us; the launch traced here: 292 us
  blocking collectives  119 us (40%)
  matrix products  76 us (26%)
  waiting for transfers between devices  31.6 us (11%)
  other arithmetic  23.8 us (8%)
  starting transfers between devices  22.9 us (8%)
  local copies, waits for them, and re-layouts  16.5 us (6%)
    psum x16, blocking collectives, by_axis(): return functools.reduce(lax.psum, axes, shard)  119 us
    dot_general x3, matrix products, on_device(): jnp.einsum('tij,tkj->tki', tile_values, picked, precision=highest)  72.7 us
    all_to_all x3, waiting for transfers between devices, on_device(): lax.all_to_all(outgoing, ROWS, split_axis=0, concat_axis=0, tiled=True)  26.1 us
    another operation x18, other arithmetic  13.9 us
    all_to_all x3, starting transfers between devices, on_device(): lax.all_to_all(outgoing, ROWS, split_axis=0, concat_axis=0, tiled=True)  12.7 us
    all_to_all x1, starting transfers between devices, on_device(): lax.all_to_all(own_requests, ROWS, split_axis=0, concat_axis=0, tiled=True)  10.1 us
  transfers between devices with their start and end apart: 4, of which 4 were waited for; matrix products, arithmetic and copies ran while one was open for 2% of the time, Pallas kernels for 0%

commit v1 on v0

v1 whole, which is shorter than its diff:
```python
import functools

import jax
import jax.numpy as jnp
from jax import lax
from jax.experimental import pallas as pl
from jax.experimental.pallas import tpu as pltpu
from jax.sharding import Mesh
from jax.sharding import PartitionSpec as P

ITERS = 3
NRHS = 4
ROWS = ("rows_0", "rows_1", "rows_2", "rows_3")
EPSILON = 1e-06

CHUNK = 16
BUFFERS = 4
UNROLL = 26
PART = 13
TOTALS = 8
MIB = 1 << 20

WW = 3
GRAM = 4

VMEM = pl.BlockSpec(memory_space=pltpu.VMEM)
SMEM = pl.BlockSpec(memory_space=pltpu.SMEM)
HBM = pl.BlockSpec(memory_space=pltpu.HBM)


def split2(x):
    high = x.astype(jnp.bfloat16)
    return high, (x - high.astype(jnp.float32)).astype(jnp.bfloat16)


def prepare_kernel(count, tiles, weights, done, buffer, arrived, packed, left):
    chunks = tiles.shape[0] // CHUNK
    pairs = CHUNK // 2

    def fetch(chunk):
        slot = lax.rem(chunk, BUFFERS)
        return pltpu.make_async_copy(
            tiles.at[pl.ds(chunk * CHUNK, CHUNK)], buffer.at[slot], arrived.at[slot]
        )

    def put(chunk):
        slot = lax.rem(chunk, 2)
        return pltpu.make_async_copy(
            packed.at[slot], weights.at[pl.ds(chunk * pairs, pairs)], left.at[slot]
        )

    for chunk in range(BUFFERS - 1):
        fetch(chunk).start()
    done[...] = jnp.zeros_like(done)
    live = count[0]

    def body(chunk, carry):
        @pl.when(chunk + BUFFERS - 1 < chunks)
        def _():
            fetch(chunk + BUFFERS - 1).start()

        @pl.when(chunk >= 2)
        def _():
            put(chunk - 2).wait()

        fetch(chunk).wait()
        slot = lax.rem(chunk, BUFFERS)
        target = lax.rem(chunk, 2)
        for local in range(CHUNK):
            tile = buffer[slot, local]
            tile = jnp.where(chunk * CHUNK + local < live, tile, 0.0)
            high, low = split2(tile.T)
            lanes = pl.ds((local % 2) * 128, 128)
            packed[target, local // 2, pl.ds(0, 128), lanes] = high
            packed[target, local // 2, pl.ds(128, 128), lanes] = low
        put(chunk).start()
        return carry

    lax.fori_loop(0, chunks, body, 0)
    put(chunks - 2).wait()
    put(chunks - 1).wait()


def lane_sums(terms):
    lane = lax.broadcasted_iota(jnp.int32, (8, 128), 1)
    row = jnp.zeros((8, 128), jnp.float32)
    for place, term in terms.items():
        partial = jnp.sum(term[:8] + term[8:], axis=1, keepdims=True)
        row = row + jnp.where(lane == place, partial, 0.0)
    return jnp.sum(row, axis=0, keepdims=True)


def write_outgoing(outgoing, onehot, blocks, sums):
    wide = jnp.concatenate(blocks, axis=1)
    first = wide.astype(jnp.bfloat16)
    rest = wide - first.astype(jnp.float32)
    second, third = split2(rest)
    parts = jnp.concatenate([first, second, third], axis=0)
    hot = onehot[:, :16]
    chosen = jnp.dot(
        jnp.concatenate([hot, hot, hot], axis=1), parts, preferred_element_type=jnp.float32
    )
    devices = onehot.shape[0]
    stride = NRHS + 1
    for system in range(NRHS):
        outgoing[pl.ds(system, devices, stride=stride), :] = chosen[
            :, system * 128 : (system + 1) * 128
        ]
    outgoing[pl.ds(NRHS, devices, stride=stride), :] = jnp.broadcast_to(sums, (devices, 128))


def first_kernel(right_side, asked, prepared, onehot, outgoing):
    del prepared
    lane = lax.broadcasted_iota(jnp.int32, asked.shape, 1)
    hot = (asked[...] == lane).astype(jnp.float32).astype(jnp.bfloat16)
    onehot[...] = hot
    blocks = [right_side[pl.ds(k, 16, stride=NRHS), :] for k in range(NRHS)]
    sums = lane_sums({WW * NRHS + k: blocks[k] * blocks[k] for k in range(NRHS)})
    write_outgoing(outgoing, hot, blocks, sums)


def coefficients(rows, system):
    def entry(row, group):
        place = group * NRHS + system
        return jnp.broadcast_to(row[:, place : place + 1], (1, 128))

    beta = jnp.sqrt(entry(rows[0], WW) + EPSILON)
    columns = []
    gram = {}
    for column, row in enumerate(rows[1:]):
        dots = [entry(row, i) for i in range(column + 1)]
        for i in range(column + 1):
            gram[i, column] = gram[column, i] = entry(row, GRAM + i)
        h = []
        for i in range(column + 1):
            value = dots[i]
            for l in range(i):
                value = value - h[l] * gram[l, i]
            h.append(value)
        left = entry(row, WW)
        for i in range(column + 1):
            left = left - h[i] * dots[i]
        for i in range(column + 1):
            residue = dots[i]
            for l in range(column + 1):
                residue = residue - h[l] * gram[l, i]
            left = left - h[i] * residue
        columns.append((h, jnp.sqrt(jnp.maximum(left, 0.0) + EPSILON)))
    return beta, columns


def step_kernel(step, last, *refs):
    refs = list(refs)
    slots, rows_of, stored, onehot, incoming, own = refs[:6]
    del refs[:6]
    earlier_sums = refs[:step]
    del refs[:step]
    earlier = refs[:step]
    del refs[:step]
    basis, sums_out, product, outgoing = refs[:4]
    del refs[:4]
    parts = stored.shape[0] // PART
    weights = stored
    if step == 0:
        weights, arrived = refs.pop(0), refs.pop()

        def fetch(part):
            place = pl.ds(part * PART, PART)
            return pltpu.make_async_copy(stored.at[place], weights.at[place], arrived.at[part])

        for part in range(parts):
            fetch(part).start()
    table, *totals = refs
    devices = onehot.shape[0]
    blocks = 16
    all_blocks = blocks + devices
    stride = NRHS + 1

    sums = jnp.sum(incoming[pl.ds(NRHS, devices, stride=stride), :], axis=0, keepdims=True)
    sums_out[...] = jnp.broadcast_to(sums, (8, 128))
    sums_rows = [ref[pl.ds(0, 1), :] for ref in earlier_sums] + [sums]
    for total in totals:
        total[...] = jnp.zeros_like(total)
    for k in range(NRHS):
        beta, columns = coefficients(sums_rows, k)
        if step == 0:
            scale = 1.0 / beta
            mine = own[pl.ds(k, blocks, stride=NRHS), :]
            h = []
        else:
            h, length = columns[-1]
            scale = 1.0 / length
            mine = own[pl.ds(k * blocks, blocks), :]
        theirs = incoming[pl.ds(k, devices, stride=stride), :]
        for start, size, value in ((0, blocks, mine), (blocks, devices, theirs)):
            for i in range(step):
                value = value - h[i] * earlier[i][pl.ds(k * all_blocks + start, size), :]
            value = value * scale
            basis[pl.ds(k * all_blocks + start, size), :] = value
            high = value.astype(jnp.bfloat16).astype(jnp.float32)
            table[pl.ds(start * 8 + k, size, stride=8), :] = high
            table[pl.ds(start * 8 + NRHS + k, size, stride=8), :] = value - high

    pairs = weights.shape[0]

    def body(trip, carry):
        for local in range(UNROLL):
            pair = trip * UNROLL + local
            if step == 0 and local % PART == 0:
                fetch(trip * (UNROLL // PART) + local // PART).wait()
            picked = [
                table[pl.ds(pl.multiple_of(slots[2 * pair + side] * 8, 8), 8), :]
                for side in range(2)
            ]
            left = jnp.concatenate(picked, axis=0).astype(jnp.bfloat16)
            left = jnp.concatenate([left, left], axis=1)
            result = jnp.dot(left, weights[pair], preferred_element_type=jnp.float32)
            for side in range(2):
                total = totals[(2 * local + side) % TOTALS]
                place = pl.ds(pl.multiple_of(rows_of[2 * pair + side] * 8, 8), 8)
                total[place, :] += result[side * 8 : side * 8 + 8, side * 128 : side * 128 + 128]
        return carry

    lax.fori_loop(0, pairs // UNROLL, body, 0)

    total = totals[0]
    summed = total[...]
    for other in totals[1:]:
        summed = summed + other[...]
    total[...] = summed
    new = [
        total[pl.ds(k, blocks, stride=8), :] + total[pl.ds(NRHS + k, blocks, stride=8), :]
        for k in range(NRHS)
    ]
    terms = {}
    for k in range(NRHS):
        product[pl.ds(k * blocks, blocks), :] = new[k]
        latest = basis[pl.ds(k * all_blocks, blocks), :]
        known = [ref[pl.ds(k * all_blocks, blocks), :] for ref in earlier] + [latest]
        for i, vector in enumerate(known):
            terms[i * NRHS + k] = vector * new[k]
            terms[(GRAM + i) * NRHS + k] = vector * latest
        terms[WW * NRHS + k] = new[k] * new[k]
    local = lane_sums(terms)
    if last:
        outgoing[...] = jnp.broadcast_to(local, outgoing.shape)
    else:
        write_outgoing(outgoing, onehot[...], new, local)


def weights_of(beta, columns):
    rotations = []
    triangle = []
    target = [beta]
    for column, (h, length) in enumerate(columns):
        values = list(h) + [length]
        for earlier, (cosine, sine) in enumerate(rotations):
            first, second = values[earlier], values[earlier + 1]
            values[earlier] = cosine * first + sine * second
            values[earlier + 1] = cosine * second - sine * first
        first, second = values[column], values[column + 1]
        radius = jnp.sqrt(first * first + second * second)
        cosine, sine = first / radius, second / radius
        rotations.append((cosine, sine))
        triangle.append(values[:column] + [radius])
        leading = target[column]
        target[column] = cosine * leading
        target.append(-sine * leading)
    size = len(columns)
    weights = [None] * size
    for column in reversed(range(size)):
        value = target[column]
        for later in range(column + 1, size):
            value = value - triangle[later][column] * weights[later]
        weights[column] = value / triangle[column][column]
    return weights


def final_kernel(incoming, sums0, sums1, sums2, basis0, basis1, basis2, solution, hessenberg):
    blocks = 16
    all_blocks = basis0.shape[0] // NRHS
    sums = jnp.sum(incoming[...], axis=0, keepdims=True)
    rows = [ref[pl.ds(0, 1), :] for ref in (sums0, sums1, sums2)] + [sums]
    row_id = lax.broadcasted_iota(jnp.int32, (8, 128), 0)
    lane = lax.broadcasted_iota(jnp.int32, (8, 128), 1)
    tables = [jnp.zeros((8, 128), jnp.float32)] * ITERS
    for k in range(NRHS):
        beta, columns = coefficients(rows, k)
        weights = weights_of(beta, columns)
        value = jnp.zeros((blocks, 128), jnp.float32)
        for weight, basis in zip(weights, (basis0, basis1, basis2)):
            value = value + weight * basis[pl.ds(k * all_blocks, blocks), :]
        solution[pl.ds(k, blocks, stride=NRHS), :] = value
        for column, (h, length) in enumerate(columns):
            for i, entry in enumerate(list(h) + [length]):
                tables[column] = jnp.where((row_id == k) & (lane == i), entry, tables[column])
    for column in range(ITERS):
        hessenberg[column] = tables[column][:NRHS, : ITERS + 1]


def params(limit):
    return pltpu.CompilerParams(vmem_limit_bytes=limit * MIB)


def exchange(outgoing):
    size = outgoing.shape[0]
    moved = lax.all_to_all(
        outgoing.reshape(size, 1, 128), ROWS, split_axis=0, concat_axis=0, tiled=True
    )
    return moved.reshape(size, 128)


def on_device(tile_values, tile_row, tile_slot, tile_count, requests, right_side):
    devices = lax.axis_size(ROWS)
    tiles = tile_values.shape[0]
    blocks = right_side.shape[0]
    all_blocks = blocks + devices
    f32 = jnp.float32
    flat = right_side.reshape(blocks * NRHS, 128)
    asked = exchange(jnp.broadcast_to(requests[0], (devices, 128)))
    weights, prepared = pl.pallas_call(
        prepare_kernel,
        out_shape=(
            pltpu.HBM((tiles // 2, 256, 256), jnp.bfloat16),
            jax.ShapeDtypeStruct((8, 128), f32),
        ),
        in_specs=[SMEM, HBM],
        out_specs=(HBM, VMEM),
        scratch_shapes=[
            pltpu.VMEM((BUFFERS, CHUNK, 128, 128), f32),
            pltpu.SemaphoreType.DMA((BUFFERS,)),
            pltpu.VMEM((2, CHUNK // 2, 256, 256), jnp.bfloat16),
            pltpu.SemaphoreType.DMA((2,)),
        ],
        compiler_params=params(24),
        cost_estimate=pl.CostEstimate(
            flops=100_000_000, bytes_accessed=tiles * 65536, transcendentals=0
        ),
        name="prepare",
    )(tile_count, pltpu.with_memory_space_constraint(tile_values, pltpu.HBM))
    onehot, outgoing = pl.pallas_call(
        first_kernel,
        out_shape=(
            jax.ShapeDtypeStruct((devices, 128), jnp.bfloat16),
            jax.ShapeDtypeStruct((devices * (NRHS + 1), 128), f32),
        ),
        in_specs=[VMEM, VMEM, VMEM],
        out_specs=(VMEM, VMEM),
        compiler_params=params(8),
        name="first",
    )(flat, asked, prepared)
    sums, basis = [], []
    own = flat
    for step in range(ITERS):
        last = step == ITERS - 1
        incoming = exchange(outgoing)
        shapes = [
            jax.ShapeDtypeStruct((NRHS * all_blocks, 128), f32),
            jax.ShapeDtypeStruct((8, 128), f32),
            jax.ShapeDtypeStruct((NRHS * blocks, 128), f32),
            jax.ShapeDtypeStruct((devices if last else devices * (NRHS + 1), 128), f32),
        ]
        scratch = [pltpu.VMEM((all_blocks * 8, 128), f32)]
        scratch += [pltpu.VMEM((blocks * 8, 128), f32)] * TOTALS
        if step == 0:
            shapes.append(pltpu.VMEM(weights.shape, weights.dtype))
            scratch.append(pltpu.SemaphoreType.DMA((weights.shape[0] // PART,)))
            weights = pltpu.with_memory_space_constraint(weights, pltpu.HBM)
        vector, row, own, outgoing, *kept = pl.pallas_call(
            functools.partial(step_kernel, step, last),
            out_shape=shapes,
            in_specs=[SMEM, SMEM, HBM if step == 0 else VMEM] + [VMEM] * (3 + 2 * step),
            out_specs=[VMEM] * len(shapes),
            scratch_shapes=scratch,
            compiler_params=params(24),
            name=f"step{step}",
        )(tile_slot, tile_row, weights, onehot, incoming, own, *sums, *basis)
        if kept:
            weights = kept[0]
        sums.append(row)
        basis.append(vector)
    incoming = exchange(outgoing)
    solution, hessenberg = pl.pallas_call(
        final_kernel,
        out_shape=(
            jax.ShapeDtypeStruct((blocks * NRHS, 128), f32),
            jax.ShapeDtypeStruct((ITERS, NRHS, ITERS + 1), f32),
        ),
        in_specs=[VMEM] * (1 + 2 * ITERS),
        out_specs=(VMEM, VMEM),
        compiler_params=params(8),
        name="final",
    )(incoming, *sums, *basis)
    return solution.reshape(blocks, NRHS, 128), hessenberg.transpose(1, 2, 0)


def solution(mesh):
    finer = Mesh(mesh.devices.reshape(4, 4, 4, 2), ROWS)
    placed = (
        P(ROWS, None, None),
        P(ROWS),
        P(ROWS),
        P(ROWS),
        P(ROWS, None, None),
        P(ROWS, None, None),
    )
    return jax.shard_map(
        on_device,
        mesh=finer,
        in_specs=placed,
        out_specs=(P(ROWS, None, None), P()),
        check_vma=False,
    )
```

time: 296 us -> 107 us (0.36); the launches traced: 292 us -> 107 us
  matrix products: 76 us -> 0 us
  blocking collectives: 119 us -> 67.1 us
  waiting for transfers between devices: 31.6 us -> 0.01 us
  Pallas kernels: 0 us -> 25.1 us
  other arithmetic: 23.8 us -> 0 us
  local copies, waits for them, and re-layouts: 16.5 us -> 1.52 us
  starting transfers between devices: 22.9 us -> 11.5 us
    psum x16 -> x0, blocking collectives: 119 us -> none  [by_axis(): return functools.reduce(lax.psum, axes, shard)]
    dot_general x10 -> x0, matrix products: 76 us -> none  [the longest x3 72.7 us: on_device(): jnp.einsum('tij,tkj->tki', tile_values, picked, precision=highest)]
    all_to_all x0 -> x4, blocking collectives: none -> 67.1 us  [exchange(): lax.all_to_all(outgoing.reshape(size, 1, 128), ROWS, split_axis=0, concat...]
    all_to_all x4 -> x1, waiting for transfers between devices: 31.6 us -> 0.01 us  [exchange(): lax.all_to_all(outgoing.reshape(size, 1, 128), ROWS, split_axis=0, concat...]
    pallas_call x0 -> x6, Pallas kernels: none -> 25.1 us  [the longest x3 13.3 us: on_device(): pl.pallas_call(functools.partial(step_kernel, step, last), out_shape=shap...]
    another operation x21 -> x0, other arithmetic: 14 us -> none
    all_to_all x4 -> x1, starting transfers between devices: 22.9 us -> 11.5 us  [exchange(): lax.all_to_all(outgoing.reshape(size, 1, 128), ROWS, split_axis=0, concat...]
    gather x6 -> x0, local copies, waits for them, and re-layouts: 7 us -> none  [the longest x3 4.28 us: on_device(): vector[asked_blocks].reshape(devices, -1, vector.shape[1], vector.shape[2])]
  transfers between devices with their start and end apart: 4 -> 1, of which waited for: 4 -> 0; matrix products, arithmetic and copies ran while one was open for 2% -> 0% of each run, Pallas kernels for 0% -> 10%
where the time goes in v1:
time: 107 us
  blocking collectives  67.1 us (63%)
  Pallas kernels  25.1 us (23%)
  starting transfers between devices  11.5 us (11%)
  local copies, waits for them, and re-layouts  1.52 us (1%)
  between operations  1.36 us (1%)
    all_to_all x4, blocking collectives, exchange(): lax.all_to_all(outgoing.reshape(size, 1, 128), ROWS, split_axis=0, concat...  67.1 us
    pallas_call x3, Pallas kernels, on_device(): pl.pallas_call(functools.partial(step_kernel, step, last), out_shape=shap...  13.3 us
    all_to_all x1, starting transfers between devices, exchange(): lax.all_to_all(outgoing.reshape(size, 1, 128), ROWS, split_axis=0, concat...  11.5 us
    pallas_call x1, Pallas kernels, on_device(): pl.pallas_call(prepare_kernel, out_shape=(pltpu.HBM((tiles // 2, 256, 256...  10.7 us
  transfers between devices with their start and end apart: 1, of which 0 were waited for; matrix products, arithmetic and copies ran while one was open for 0% of the time, Pallas kernels for 10%

profile of v1, /device:TPU:1, one launch (start us, length us, event | category | flops | bytes accessed | tf_op | source)
XLA Modules:
  0.0 106.6 jit_solution(15639564312711396182)
XLA Ops:
  0.6 0.0 copy-start
  0.6 0.0 copy-start.1
  0.7 0.0 copy-start.2
  0.7 1.5 %reshape.42 = s32[128,1,128]{2,1,0:T(1,128)} broadcast(s32[128]{0:T(128)} %bitcast.32), dimensions={0} | broadcast | bytes 66048 | tf_op jit(solution)/shard_map/reshape | solution.py:308
  2.2 11.5 %all-to-all-start = ((s32[128,1,128]{2,1,0:T(1,128)}), s32[128,1,128]{2,1,0:T(1,128)S(1)}, u32[]{:S(2)}, u32[]{:S(2)}) async-start(s32[128,1,128]{2,1,0:T(1,128)} %reshape.42), calls=%async_computation | async-start | bytes 131072 | tf_op jit(solution)/shard_map/all_to_all | solution.py:307
  14.3 10.7 %prepare.1 = (bf16[104,256,256]{2,1,0:T(8,128)(2,1)}, f32[8,128]{1,0:T(8,128)S(1)}) custom-call(s32[1]{0:T(128)S(6)} %copy.12.count, f32[208,128,128]{2,1,0:T(8,128)} %tiles.1), custom_call_target="tpu_custom_call" | custom-call | flops 100000000 | bytes 13631488 | tf_op jit(solution)/shard_map/prepare/pallas_call | solution.py:321
  25.0 0.0 all-to-all-done
  25.0 0.0 copy-done
  25.0 0.2 first.1
  25.3 21.0 %all_to_all.25 = f32[640,1,128]{2,1,0:T(1,128)S(1)} all-to-all(f32[640,1,128]{2,1,0:T(1,128)S(1)} %bitcast.26), channel_id=1, replica_groups=mesh['rows_0'=4,'rows_1'=4,'rows_2'=4,'rows_3'=2] {'rows_0','rows_1','ro..., dimensions={0} | all-to-all | bytes 655360 | tf_op jit(solution)/shard_map/all_to_all | solution.py:307
  46.2 0.0 copy-done.1
  46.2 0.0 copy-done.2
  46.2 6.1 %step0.1 = (f32[576,128]{1,0:T(8,128)S(1)}, f32[8,128]{1,0:T(8,128)S(1)}, f32[64,128]{1,0:T(8,128)S(1)}, f32[640,128]{1,0:T(8,128)S(1)}, bf16[104,256,256]{2,1,0:T(8,128)(2,1)S(1)}) custom-call(s32[208]{0:T(256)S(1)} %copy-done.1, s32[208]{0:T(256)S(1)} %copy-done.2, bf16[104,256,256]{2,1,0:T(8,128)(2,1)} %get-tuple-element.20.refs_2_, ...), custom_call_target="tpu_custom_call" | custom-call | tf_op jit(solution)/shard_map/step0/pallas_call | solution.py:369
  52.4 16.0 %all_to_all.26 = f32[640,1,128]{2,1,0:T(1,128)S(1)} all-to-all(f32[640,1,128]{2,1,0:T(1,128)S(1)} %bitcast.24), channel_id=1, replica_groups=mesh['rows_0'=4,'rows_1'=4,'rows_2'=4,'rows_3'=2] {'rows_0','rows_1','ro..., dimensions={0} | all-to-all | bytes 655360 | tf_op jit(solution)/shard_map/all_to_all | solution.py:307
  68.4 3.4 %step1.1 = (f32[576,128]{1,0:T(8,128)S(1)}, f32[8,128]{1,0:T(8,128)S(1)}, f32[64,128]{1,0:T(8,128)S(1)}, f32[640,128]{1,0:T(8,128)S(1)}) custom-call(s32[208]{0:T(256)S(1)} %copy-done.1, s32[208]{0:T(256)S(1)} %copy-done.2, bf16[104,256,256]{2,1,0:T(8,128)(2,1)S(1)} %get-tuple-element.24.refs_2_, bf16[128,128]{1,0:T(8,128)(2,1)S(1)} %get-tuple-element.22.refs_3_, ...), custom_call_target="tpu_custom_call" | custom-call | tf_op jit(solution)/shard_map/step1/pallas_call | solution.py:369
  71.7 16.0 %all_to_all.27 = f32[640,1,128]{2,1,0:T(1,128)S(1)} all-to-all(f32[640,1,128]{2,1,0:T(1,128)S(1)} %bitcast.25), channel_id=1, replica_groups=mesh['rows_0'=4,'rows_1'=4,'rows_2'=4,'rows_3'=2] {'rows_0','rows_1','ro..., dimensions={0} | all-to-all | bytes 655360 | tf_op jit(solution)/shard_map/all_to_all | solution.py:307
  87.7 3.9 %step2.1 = (f32[576,128]{1,0:T(8,128)S(1)}, f32[8,128]{1,0:T(8,128)S(1)}, f32[64,128]{1,0:T(8,128)}, f32[128,128]{1,0:T(8,128)S(1)}) custom-call(s32[208]{0:T(256)S(1)} %copy-done.1, s32[208]{0:T(256)S(1)} %copy-done.2, bf16[104,256,256]{2,1,0:T(8,128)(2,1)S(1)} %get-tuple-element.24.refs_2_, bf16[128,128]{1,0:T(8,128)(2,1)S(1)} %get-tuple-element.22.refs_3_, ...), custom_call_target="tpu_custom_call" | custom-call | tf_op jit(solution)/shard_map/step2/pallas_call | solution.py:369
  91.6 14.1 %all_to_all.28 = f32[128,1,128]{2,1,0:T(1,128)S(1)} all-to-all(f32[128,1,128]{2,1,0:T(1,128)S(1)} %bitcast.31), channel_id=1, replica_groups=mesh['rows_0'=4,'rows_1'=4,'rows_2'=4,'rows_3'=2] {'rows_0','rows_1','ro..., dimensions={0} | all-to-all | bytes 131072 | tf_op jit(solution)/shard_map/all_to_all | solution.py:307
  105.7 0.9 final.1
Async XLA Ops:
  0.6 24.4 %copy-start = (f32[16,4,128]{2,1,0:T(4,128)S(1)}, f32[16,4,128]{2,1,0:T(4,128)}, u32[]{:S(2)}) copy-start(f32[16,4,128]{2,1,0:T(4,128)} %param.11) | copy-start | bytes 98308
  0.6 45.6 %copy-start.1 = (s32[208]{0:T(256)S(1)}, s32[208]{0:T(256)}, u32[]{:S(2)}) copy-start(s32[208]{0:T(256)} %refs_0_.5) | copy-start | bytes 2500
  0.7 45.6 %copy-start.2 = (s32[208]{0:T(256)S(1)}, s32[208]{0:T(256)}, u32[]{:S(2)}) copy-start(s32[208]{0:T(256)} %refs_1_.5) | copy-start | bytes 2500
  2.2 22.8 %all-to-all-start = ((s32[128,1,128]{2,1,0:T(1,128)}), s32[128,1,128]{2,1,0:T(1,128)S(1)}, u32[]{:S(2)}, u32[]{:S(2)}) async-start(s32[128,1,128]{2,1,0:T(1,128)} %reshape.42), calls=%async_computation | async-start | bytes 131072 | tf_op jit(solution)/shard_map/all_to_all | solution.py:307

commit v2 on v1

--- a/solution.py
+++ b/solution.py
@@ -16,7 +16,6 @@
 CHUNK = 16
 BUFFERS = 4
 UNROLL = 26
-PART = 13
 TOTALS = 8
 MIB = 1 << 20
 
@@ -31,54 +30,6 @@
 def split2(x):
     high = x.astype(jnp.bfloat16)
     return high, (x - high.astype(jnp.float32)).astype(jnp.bfloat16)
-
-
-def prepare_kernel(count, tiles, weights, done, buffer, arrived, packed, left):
-    chunks = tiles.shape[0] // CHUNK
-    pairs = CHUNK // 2
-
-    def fetch(chunk):
-        slot = lax.rem(chunk, BUFFERS)
-        return pltpu.make_async_copy(
-            tiles.at[pl.ds(chunk * CHUNK, CHUNK)], buffer.at[slot], arrived.at[slot]
-        )
-
-    def put(chunk):
-        slot = lax.rem(chunk, 2)
-        return pltpu.make_async_copy(
-            packed.at[slot], weights.at[pl.ds(chunk * pairs, pairs)], left.at[slot]
-        )
-
-    for chunk in range(BUFFERS - 1):
-        fetch(chunk).start()
-    done[...] = jnp.zeros_like(done)
-    live = count[0]
-
-    def body(chunk, carry):
-        @pl.when(chunk + BUFFERS - 1 < chunks)
-        def _():
-            fetch(chunk + BUFFERS - 1).start()
-
-        @pl.when(chunk >= 2)
-        def _():
-            put(chunk - 2).wait()
-
-        fetch(chunk).wait()
-        slot = lax.rem(chunk, BUFFERS)
-        target = lax.rem(chunk, 2)
-        for local in range(CHUNK):
-            tile = buffer[slot, local]
-            tile = jnp.where(chunk * CHUNK + local < live, tile, 0.0)
-            high, low = split2(tile.T)
-            lanes = pl.ds((local % 2) * 128, 128)
-            packed[target, local // 2, pl.ds(0, 128), lanes] = high
-            packed[target, local // 2, pl.ds(128, 128), lanes] = low
-        put(chunk).start()
-        return carry
-
-    lax.fori_loop(0, chunks, body, 0)
-    put(chunks - 2).wait()
-    put(chunks - 1).wait()
 
 
 def lane_sums(terms):
@@ -109,12 +60,32 @@
     outgoing[pl.ds(NRHS, devices, stride=stride), :] = jnp.broadcast_to(sums, (devices, 128))
 
 
-def first_kernel(right_side, asked, prepared, onehot, outgoing):
-    del prepared
+def begin_kernel(*refs):
+    count, *given = refs[:5]
+    wanted, own, *kept = refs[5:10]
+    requests, right_side, copied = refs[10:]
+    held = (requests, right_side)
+    kept[-1][0] = count[0]
+    copies = [
+        pltpu.make_async_copy(source, target, copied.at[place])
+        for place, (source, target) in enumerate(zip(given, [*held, *kept[:2]]))
+    ]
+    for copy in copies:
+        copy.start()
+    copies[0].wait()
+    wanted[...] = jnp.broadcast_to(requests[...], wanted.shape).T
+    copies[1].wait()
+    for k in range(NRHS):
+        own[pl.ds(k * 16, 16), :] = right_side[pl.ds(k, 16, stride=NRHS), :]
+    for copy in copies[2:]:
+        copy.wait()
+
+
+def first_kernel(own, asked, onehot, outgoing):
     lane = lax.broadcasted_iota(jnp.int32, asked.shape, 1)
     hot = (asked[...] == lane).astype(jnp.float32).astype(jnp.bfloat16)
     onehot[...] = hot
-    blocks = [right_side[pl.ds(k, 16, stride=NRHS), :] for k in range(NRHS)]
+    blocks = [own[pl.ds(k * 16, 16), :] for k in range(NRHS)]
     sums = lane_sums({WW * NRHS + k: blocks[k] * blocks[k] for k in range(NRHS)})
     write_outgoing(outgoing, hot, blocks, sums)
 
@@ -151,30 +122,55 @@
 
 def step_kernel(step, last, *refs):
     refs = list(refs)
-    slots, rows_of, stored, onehot, incoming, own = refs[:6]
-    del refs[:6]
+    if step == 0:
+        count, tiles = refs[:2]
+        del refs[:2]
+    else:
+        weights = refs.pop(0)
+    slots, rows_of, onehot, incoming, own = refs[:5]
+    del refs[:5]
     earlier_sums = refs[:step]
     del refs[:step]
     earlier = refs[:step]
     del refs[:step]
     basis, sums_out, product, outgoing = refs[:4]
     del refs[:4]
-    parts = stored.shape[0] // PART
-    weights = stored
     if step == 0:
-        weights, arrived = refs.pop(0), refs.pop()
-
-        def fetch(part):
-            place = pl.ds(part * PART, PART)
-            return pltpu.make_async_copy(stored.at[place], weights.at[place], arrived.at[part])
-
-        for part in range(parts):
-            fetch(part).start()
+        weights = refs.pop(0)
+        arrived = refs.pop()
+        buffer = refs.pop()
     table, *totals = refs
     devices = onehot.shape[0]
     blocks = 16
     all_blocks = blocks + devices
     stride = NRHS + 1
+
+    if step == 0:
+        chunks = tiles.shape[0] // CHUNK
+        live = count[0]
+
+        def fetch(chunk):
+            slot = lax.rem(chunk, BUFFERS)
+            return pltpu.make_async_copy(
+                tiles.at[pl.ds(chunk * CHUNK, CHUNK)], buffer.at[slot], arrived.at[slot]
+            )
+
+        def pack(chunk):
+            slot = lax.rem(chunk, BUFFERS)
+            for local in range(CHUNK):
+                tile = buffer[slot, local]
+                tile = jnp.where(chunk * CHUNK + local < live, tile, 0.0)
+                high, low = split2(tile.T)
+                pair = chunk * (CHUNK // 2) + local // 2
+                lanes = pl.ds((local % 2) * 128, 128)
+                weights[pair, pl.ds(0, 128), lanes] = high
+                weights[pair, pl.ds(128, 128), lanes] = low
+
+        for chunk in range(BUFFERS - 1):
+            fetch(chunk).start()
+        fetch(BUFFERS - 1).start()
+        fetch(0).wait()
+        pack(0)
 
     sums = jnp.sum(incoming[pl.ds(NRHS, devices, stride=stride), :], axis=0, keepdims=True)
     sums_out[...] = jnp.broadcast_to(sums, (8, 128))
@@ -185,12 +181,11 @@
         beta, columns = coefficients(sums_rows, k)
         if step == 0:
             scale = 1.0 / beta
-            mine = own[pl.ds(k, blocks, stride=NRHS), :]
             h = []
         else:
             h, length = columns[-1]
             scale = 1.0 / length
-            mine = own[pl.ds(k * blocks, blocks), :]
+        mine = own[pl.ds(k * blocks, blocks), :]
         theirs = incoming[pl.ds(k, devices, stride=stride), :]
         for start, size, value in ((0, blocks, mine), (blocks, devices, theirs)):
             for i in range(step):
@@ -201,13 +196,9 @@
             table[pl.ds(start * 8 + k, size, stride=8), :] = high
             table[pl.ds(start * 8 + NRHS + k, size, stride=8), :] = value - high
 
-    pairs = weights.shape[0]
-
-    def body(trip, carry):
-        for local in range(UNROLL):
-            pair = trip * UNROLL + local
-            if step == 0 and local % PART == 0:
-                fetch(trip * (UNROLL // PART) + local // PART).wait()
+    def multiply(first_pair, size):
+        for local in range(size):
+            pair = first_pair + local
             picked = [
                 table[pl.ds(pl.multiple_of(slots[2 * pair + side] * 8, 8), 8), :]
                 for side in range(2)
@@ -219,9 +210,30 @@
                 total = totals[(2 * local + side) % TOTALS]
                 place = pl.ds(pl.multiple_of(rows_of[2 * pair + side] * 8, 8), 8)
                 total[place, :] += result[side * 8 : side * 8 + 8, side * 128 : side * 128 + 128]
-        return carry
-
-    lax.fori_loop(0, pairs // UNROLL, body, 0)
+
+    pairs = weights.shape[0]
+    if step == 0:
+        half = CHUNK // 2
+
+        def body(chunk, carry):
+            @pl.when(chunk + BUFFERS - 1 < chunks)
+            def _():
+                fetch(chunk + BUFFERS - 1).start()
+
+            fetch(chunk).wait()
+            pack(chunk)
+            multiply((chunk - 1) * half, half)
+            return carry
+
+        lax.fori_loop(1, chunks, body, 0)
+        multiply((chunks - 1) * half, half)
+    else:
+
+        def body(trip, carry):
+            multiply(trip * UNROLL, UNROLL)
+            return carry
+
+        lax.fori_loop(0, pairs // UNROLL, body, 0)
 
     total = totals[0]
     summed = total[...]
@@ -302,6 +314,10 @@
     return pltpu.CompilerParams(vmem_limit_bytes=limit * MIB)
 
 
+def in_hbm(array):
+    return pltpu.with_memory_space_constraint(array, pltpu.HBM)
+
+
 def exchange(outgoing):
     size = outgoing.shape[0]
     moved = lax.all_to_all(
@@ -317,40 +333,39 @@
     all_blocks = blocks + devices
     f32 = jnp.float32
     flat = right_side.reshape(blocks * NRHS, 128)
-    asked = exchange(jnp.broadcast_to(requests[0], (devices, 128)))
-    weights, prepared = pl.pallas_call(
-        prepare_kernel,
+    wanted, own, *kept = pl.pallas_call(
+        begin_kernel,
         out_shape=(
-            pltpu.HBM((tiles // 2, 256, 256), jnp.bfloat16),
-            jax.ShapeDtypeStruct((8, 128), f32),
+            jax.ShapeDtypeStruct((devices, 128), jnp.int32),
+            jax.ShapeDtypeStruct((blocks * NRHS, 128), f32),
+            pltpu.SMEM(tile_slot.shape, tile_slot.dtype),
+            pltpu.SMEM(tile_row.shape, tile_row.dtype),
+            pltpu.SMEM(tile_count.shape, tile_count.dtype),
         ),
-        in_specs=[SMEM, HBM],
-        out_specs=(HBM, VMEM),
+        in_specs=[SMEM] + [HBM] * 4,
+        out_specs=(VMEM, VMEM, SMEM, SMEM, SMEM),
         scratch_shapes=[
-            pltpu.VMEM((BUFFERS, CHUNK, 128, 128), f32),
-            pltpu.SemaphoreType.DMA((BUFFERS,)),
-            pltpu.VMEM((2, CHUNK // 2, 256, 256), jnp.bfloat16),
-            pltpu.SemaphoreType.DMA((2,)),
+            pltpu.VMEM((1, devices), jnp.int32),
+            pltpu.VMEM(flat.shape, f32),
+            pltpu.SemaphoreType.DMA((4,)),
         ],
-        compiler_params=params(24),
-        cost_estimate=pl.CostEstimate(
-            flops=100_000_000, bytes_accessed=tiles * 65536, transcendentals=0
-        ),
-        name="prepare",
-    )(tile_count, pltpu.with_memory_space_constraint(tile_values, pltpu.HBM))
+        compiler_params=params(8),
+        name="begin",
+    )(tile_count, *map(in_hbm, (requests.reshape(1, devices), flat, tile_slot, tile_row)))
+    slots, rows_of, count = kept
+    asked = exchange(wanted)
     onehot, outgoing = pl.pallas_call(
         first_kernel,
         out_shape=(
             jax.ShapeDtypeStruct((devices, 128), jnp.bfloat16),
             jax.ShapeDtypeStruct((devices * (NRHS + 1), 128), f32),
         ),
-        in_specs=[VMEM, VMEM, VMEM],
+        in_specs=[VMEM, VMEM],
         out_specs=(VMEM, VMEM),
         compiler_params=params(8),
         name="first",
-    )(flat, asked, prepared)
+    )(own, asked)
     sums, basis = [], []
-    own = flat
     for step in range(ITERS):
         last = step == ITERS - 1
         incoming = exchange(outgoing)
@@ -362,19 +377,27 @@
         ]
         scratch = [pltpu.VMEM((all_blocks * 8, 128), f32)]
         scratch += [pltpu.VMEM((blocks * 8, 128), f32)] * TOTALS
+        operands = [slots, rows_of, onehot, incoming, own, *sums, *basis]
+        specs = [SMEM, SMEM] + [VMEM] * (3 + 2 * step)
         if step == 0:
-            shapes.append(pltpu.VMEM(weights.shape, weights.dtype))
-            scratch.append(pltpu.SemaphoreType.DMA((weights.shape[0] // PART,)))
-            weights = pltpu.with_memory_space_constraint(weights, pltpu.HBM)
+            shapes.append(pltpu.VMEM((tiles // 2, 256, 256), jnp.bfloat16))
+            scratch.append(pltpu.VMEM((BUFFERS, CHUNK, 128, 128), f32))
+            scratch.append(pltpu.SemaphoreType.DMA((BUFFERS,)))
+            stored = in_hbm(tile_values)
+            operands = [count, stored] + operands
+            specs = [SMEM, HBM] + specs
+        else:
+            operands = [weights] + operands
+            specs = [VMEM] + specs
         vector, row, own, outgoing, *kept = pl.pallas_call(
             functools.partial(step_kernel, step, last),
             out_shape=shapes,
-            in_specs=[SMEM, SMEM, HBM if step == 0 else VMEM] + [VMEM] * (3 + 2 * step),
+            in_specs=specs,
             out_specs=[VMEM] * len(shapes),
             scratch_shapes=scratch,
             compiler_params=params(24),
             name=f"step{step}",
-        )(tile_slot, tile_row, weights, onehot, incoming, own, *sums, *basis)
+        )(*operands)
         if kept:
             weights = kept[0]
         sums.append(row)

time: 107 us -> 102 us (0.953)
  blocking collectives: 67.1 us -> 82.8 us
  starting transfers between devices: 11.5 us -> 0 us
  Pallas kernels: 25.1 us -> 17.4 us
  local copies, waits for them, and re-layouts: 1.52 us -> 0 us
    all_to_all x4 -> x5, blocking collectives: 67.1 us -> 82.8 us  [exchange(): lax.all_to_all(outgoing.reshape(size, 1, 128), ROWS, split_axis=0, concat...]
    all_to_all x1 -> x0, starting transfers between devices: 11.5 us -> none  [exchange(): lax.all_to_all(outgoing.reshape(size, 1, 128), ROWS, split_axis=0, concat...]
    pallas_call x1, Pallas kernels: 10.7 us -> 0.87 us  [on_device(): pl.pallas_call(begin_kernel, out_shape=(jax.ShapeDtypeStruct((devices, 12...]
    pallas_call x3, Pallas kernels: 13.3 us -> 15.4 us  [on_device(): pl.pallas_call(functools.partial(step_kernel, step, last), out_shape=shap...]
    reshape x1 -> x0, local copies, waits for them, and re-layouts: 1.51 us -> none  [exchange(): outgoing.reshape(size, 1, 128)]
  transfers between devices with their start and end apart: 1 -> 0, of which waited for: 0 -> 0; matrix products, arithmetic and copies ran while one was open for 0% -> 0% of each run, Pallas kernels for 10% -> 0%
where the time goes in v2:
time: 102 us; the launch traced here: 101 us
  blocking collectives  82.8 us (81%)
  Pallas kernels  17.4 us (17%)
  between operations  1.31 us (1%)
    all_to_all x5, blocking collectives, exchange(): lax.all_to_all(outgoing.reshape(size, 1, 128), ROWS, split_axis=0, concat...  82.8 us
    pallas_call x3, Pallas kernels, on_device(): pl.pallas_call(functools.partial(step_kernel, step, last), out_shape=shap...  15.4 us

profile of v2, /device:TPU:1, one launch (start us, length us, event | category | flops | bytes accessed | tf_op | source)
XLA Modules:
  0.0 101.5 jit_solution(5096812790014731374)
XLA Ops:
  1.3 0.9 begin.1
  2.2 20.8 %all_to_all.25 = s32[128,1,128]{2,1,0:T(1,128)S(1)} all-to-all(s32[128,1,128]{2,1,0:T(1,128)S(1)} %bitcast.33), channel_id=1, replica_groups=mesh['rows_0'=4,'rows_1'=4,'rows_2'=4,'rows_3'=2] {'rows_0','rows_1','ro..., dimensions={0} | all-to-all | bytes 131072 | tf_op jit(solution)/shard_map/all_to_all | solution.py:323
  23.0 0.2 first.1
  23.2 15.8 %all_to_all.26 = f32[640,1,128]{2,1,0:T(1,128)S(1)} all-to-all(f32[640,1,128]{2,1,0:T(1,128)S(1)} %bitcast.29), channel_id=1, replica_groups=mesh['rows_0'=4,'rows_1'=4,'rows_2'=4,'rows_3'=2] {'rows_0','rows_1','ro..., dimensions={0} | all-to-all | bytes 655360 | tf_op jit(solution)/shard_map/all_to_all | solution.py:323
  39.0 9.4 %step0.1 = (f32[576,128]{1,0:T(8,128)S(1)}, f32[8,128]{1,0:T(8,128)S(1)}, f32[64,128]{1,0:T(8,128)S(1)}, f32[640,128]{1,0:T(8,128)S(1)}, bf16[104,256,256]{2,1,0:T(8,128)(2,1)S(1)}) custom-call(s32[1]{0:T(128)S(4)} %get-tuple-element.23.refs_0_, f32[208,128,128]{2,1,0:T(8,128)} %refs_1_.1, s32[208]{0:T(256)S(4)} %get-tuple-element.24.refs_2_.refs_1_, ...), custom_call_target="tpu_custom_call" | custom-call | tf_op jit(solution)/shard_map/step0/pallas_call | solution.py:392
  48.4 16.0 %all_to_all.27 = f32[640,1,128]{2,1,0:T(1,128)S(1)} all-to-all(f32[640,1,128]{2,1,0:T(1,128)S(1)} %bitcast.27), channel_id=1, replica_groups=mesh['rows_0'=4,'rows_1'=4,'rows_2'=4,'rows_3'=2] {'rows_0','rows_1','ro..., dimensions={0} | all-to-all | bytes 655360 | tf_op jit(solution)/shard_map/all_to_all | solution.py:323
  64.4 2.8 %step1.1 = (f32[576,128]{1,0:T(8,128)S(1)}, f32[8,128]{1,0:T(8,128)S(1)}, f32[64,128]{1,0:T(8,128)S(1)}, f32[640,128]{1,0:T(8,128)S(1)}) custom-call(bf16[104,256,256]{2,1,0:T(8,128)(2,1)S(1)} %get-tuple-element.30.refs_0_, s32[208]{0:T(256)S(4)} %get-tuple-element.24.refs_2_.refs_1_, s32[208]{0:T(256)S(4)} %get-tuple-element.25.refs_3_.refs_2_, ...), custom_call_target="tpu_custom_call" | custom-call | tf_op jit(solution)/shard_map/step1/pallas_call | solution.py:392
  67.2 16.0 %all_to_all.28 = f32[640,1,128]{2,1,0:T(1,128)S(1)} all-to-all(f32[640,1,128]{2,1,0:T(1,128)S(1)} %bitcast.28), channel_id=1, replica_groups=mesh['rows_0'=4,'rows_1'=4,'rows_2'=4,'rows_3'=2] {'rows_0','rows_1','ro..., dimensions={0} | all-to-all | bytes 655360 | tf_op jit(solution)/shard_map/all_to_all | solution.py:323
  83.2 3.3 %step2.1 = (f32[576,128]{1,0:T(8,128)S(1)}, f32[8,128]{1,0:T(8,128)S(1)}, f32[64,128]{1,0:T(8,128)}, f32[128,128]{1,0:T(8,128)S(1)}) custom-call(bf16[104,256,256]{2,1,0:T(8,128)(2,1)S(1)} %get-tuple-element.30.refs_0_, s32[208]{0:T(256)S(4)} %get-tuple-element.24.refs_2_.refs_1_, s32[208]{0:T(256)S(4)} %get-tuple-element.25.refs_3_.refs_2_, ...), custom_call_target="tpu_custom_call" | custom-call | tf_op jit(solution)/shard_map/step2/pallas_call | solution.py:392
  86.5 14.1 %all_to_all.29 = f32[128,1,128]{2,1,0:T(1,128)S(1)} all-to-all(f32[128,1,128]{2,1,0:T(1,128)S(1)} %bitcast.32), channel_id=1, replica_groups=mesh['rows_0'=4,'rows_1'=4,'rows_2'=4,'rows_3'=2] {'rows_0','rows_1','ro..., dimensions={0} | all-to-all | bytes 131072 | tf_op jit(solution)/shard_map/all_to_all | solution.py:323
  100.6 0.9 final.1

commit v3 on v2

v3 whole, which is shorter than its diff:
```python
import functools

import jax
import jax.numpy as jnp
from jax import lax
from jax.experimental import pallas as pl
from jax.experimental.pallas import tpu as pltpu
from jax.sharding import Mesh
from jax.sharding import PartitionSpec as P

ITERS = 3
NRHS = 4
BLOCKS = 16
STRIDE = NRHS + 1
LEAD = 8
ROWS = ("rows_0", "rows_1", "rows_2", "rows_3")
EPSILON = 1e-06

CHUNK = 26
BUFFERS = 4
TOTALS = 8
MIB = 1 << 20

WW = 3
GRAM = 4

VMEM = pl.BlockSpec(memory_space=pltpu.VMEM)
SMEM = pl.BlockSpec(memory_space=pltpu.SMEM)
HBM = pl.BlockSpec(memory_space=pltpu.HBM)


def row_of(shape=(8, 128)):
    return lax.broadcasted_iota(jnp.int32, shape, 0)


def lane_of(shape=(8, 128)):
    return lax.broadcasted_iota(jnp.int32, shape, 1)


def split2(x):
    high = x.astype(jnp.bfloat16)
    return high, (x - high.astype(jnp.float32)).astype(jnp.bfloat16)


def split3(x):
    first = x.astype(jnp.bfloat16)
    second, third = split2(x - first.astype(jnp.float32))
    return first, second, third


def block(ref, r):
    return ref[pl.ds(8 * r, 8), :]


def in_group(group):
    row, lane = row_of(), lane_of()
    return (lane // NRHS == group) & (lane % NRHS == row % NRHS)


def row_of_sums(terms):
    row = jnp.zeros((8, 128), jnp.float32)
    for group, term in terms.items():
        row = row + jnp.where(in_group(group), jnp.sum(term, axis=1, keepdims=True), 0.0)
    return jnp.sum(jnp.where(row_of() < NRHS, row, 0.0), axis=0, keepdims=True)


def write_outgoing(outgoing, places, blocks, sums):
    low_half = row_of() < NRHS
    packed = [
        jnp.where(low_half, blocks[2 * j], blocks[2 * j + 1]) for j in range(BLOCKS // 2)
    ]
    parts = list(split3(jnp.concatenate(packed, axis=0)))
    row = row_of((64, 128))
    tail = jnp.zeros((64, 128), jnp.float32)
    for place, part in enumerate(split3(sums)):
        tail = jnp.where(row == place, part.astype(jnp.float32), tail)
    parts.append(tail.astype(jnp.bfloat16))
    outgoing[...] = jnp.dot(
        places[...], jnp.concatenate(parts, axis=0), preferred_element_type=jnp.float32
    )


def begin_kernel(*refs):
    count, *given = refs[:5]
    wanted, own, *kept = refs[5:10]
    requests, right_side, copied = refs[10:]
    kept[-1][0] = count[0]
    copies = [
        pltpu.make_async_copy(source, target, copied.at[place])
        for place, (source, target) in enumerate(zip(given, [requests, right_side, *kept[:2]]))
    ]
    for copy in copies:
        copy.start()
    copies[0].wait()
    wanted[...] = jnp.broadcast_to(requests[...], wanted.shape).T
    copies[1].wait()
    low_half = row_of() < NRHS
    for j in range(BLOCKS // 2):
        both = block(right_side, j)
        turned = pltpu.roll(both, NRHS, 0)
        own[pl.ds(16 * j, 8), :] = jnp.where(low_half, both, turned)
        own[pl.ds(16 * j + 8, 8), :] = jnp.where(low_half, turned, both)
    for copy in copies[2:]:
        copy.wait()


def first_kernel(own, asked, places, outgoing):
    f32 = jnp.float32
    devices = asked.shape[0]
    rows = devices * STRIDE
    row = row_of((rows, devices))
    device = STRIDE * lane_of((rows, devices))
    spread = ((row >= device) & (row < device + STRIDE)).astype(f32).astype(jnp.bfloat16)
    ids = asked[...].astype(f32).astype(jnp.bfloat16)
    wanted = jnp.dot(spread, ids, preferred_element_type=f32)
    row = row.astype(f32)
    system = row - STRIDE * jnp.floor(row * (1.0 / STRIDE) + 0.5 / STRIDE)
    lane = lane_of((rows, 128))
    column = (lane % 64).astype(f32)
    own_block = (column == wanted * NRHS + system) & (system < NRHS)
    sums_row = (system >= NRHS) & (lane >= 64) & (lane < 67)
    places[:, :128] = own_block.astype(f32).astype(jnp.bfloat16)
    places[:, 128:] = ((own_block & (lane < 64)) | sums_row).astype(f32).astype(jnp.bfloat16)
    blocks = [block(own, r) for r in range(BLOCKS)]
    sums = row_of_sums({WW: functools.reduce(jnp.add, [b * b for b in blocks])})
    write_outgoing(outgoing, places, blocks, sums)


def coefficients(rows):
    def entry(row, group):
        chosen = jnp.where(in_group(group), row, 0.0)
        return jnp.broadcast_to(jnp.sum(chosen, axis=1, keepdims=True), (8, 128))

    beta = jnp.sqrt(entry(rows[0], WW) + EPSILON)
    columns = []
    gram = {}
    for column, row in enumerate(rows[1:]):
        dots = [entry(row, i) for i in range(column + 1)]
        for i in range(column + 1):
            gram[i, column] = gram[column, i] = entry(row, GRAM + i)
        h = []
        for i in range(column + 1):
            value = dots[i]
            for l in range(i):
                value = value - h[l] * gram[l, i]
            h.append(value)
        left = entry(row, WW)
        for i in range(column + 1):
            left = left - h[i] * dots[i]
        for i in range(column + 1):
            residue = dots[i]
            for l in range(column + 1):
                residue = residue - h[l] * gram[l, i]
            left = left - h[i] * residue
        columns.append((h, jnp.sqrt(jnp.maximum(left, 0.0) + EPSILON)))
    return beta, columns


def strided(values):
    of_system = [jnp.broadcast_to(values[k : k + 1], (8, 128)) for k in range(NRHS)]
    groups = []
    for group in range(STRIDE):
        system = (row_of() + 8 * group) % STRIDE
        chosen = of_system[NRHS - 1]
        for k in range(NRHS - 1):
            chosen = jnp.where(system == k, of_system[k], chosen)
        groups.append(chosen)
    return jnp.concatenate(groups, axis=0)


def step_kernel(step, last, *refs):
    refs = list(refs)

    def take(size):
        taken = refs[:size]
        del refs[:size]
        return taken

    count, tiles = take(2) if step == 0 else (None, None)
    packed = take(2) if step > 0 else None
    slots, rows_of, places, incoming, own = take(5)
    earlier_sums, earlier_own, earlier_halo = take(step), take(step), take(step)
    basis_own, basis_halo, sums_out, product, outgoing = take(5)
    if step == 0:
        packed = take(2)
    (table,) = take(1)
    totals = take(TOTALS)
    devices = incoming.shape[0] // STRIDE
    chunks = packed[0].shape[0] // (CHUNK * 256) * 2

    def fetch(chunk):
        slot = lax.rem(chunk, BUFFERS)
        return pltpu.make_async_copy(
            tiles.at[pl.ds(chunk * CHUNK, CHUNK)], buffer.at[slot], arrived.at[slot]
        )

    def pack(chunk, target, place):
        slot = lax.rem(chunk, BUFFERS)
        for local in range(CHUNK):
            tile = buffer[slot, local]
            tile = jnp.where(chunk * CHUNK + local < live, tile, 0.0)
            high, low = split2(tile.T)
            start = (place * CHUNK + local) * 256
            target[pl.ds(start, 128), :] = high
            target[pl.ds(start + 128, 128), :] = low

    def multiply(chunk, source, place):
        for local in range(CHUNK // 2):
            tile = chunk * CHUNK + 2 * local
            picked = [
                table[pl.ds(pl.multiple_of(slots[tile + side] * 8, 8), 8), :] for side in range(2)
            ]
            left = jnp.concatenate(picked, axis=0).astype(jnp.bfloat16)
            left = jnp.concatenate([left, left], axis=1)
            start = (place * CHUNK + 2 * local) * 256
            right = [source[pl.ds(start + side * 256, 256), :] for side in range(2)]
            result = jnp.dot(
                left, jnp.concatenate(right, axis=1), preferred_element_type=jnp.float32
            )
            for side in range(2):
                total = totals[(2 * local + side) % TOTALS]
                row = pl.ds(pl.multiple_of(rows_of[tile + side] * 8, 8), 8)
                total[row, :] += result[side * 8 : side * 8 + 8, side * 128 : side * 128 + 128]

    if step == 0:
        buffer, arrived = take(2)
        live = count[0]
        for chunk in range(BUFFERS):
            fetch(chunk).start()

    sums = jnp.sum(incoming[pl.ds(NRHS, devices, stride=STRIDE), :], axis=0, keepdims=True)
    sums_out[...] = jnp.broadcast_to(sums, (8, 128))
    beta, columns = coefficients([ref[...] for ref in earlier_sums] + [sums])
    h, length = columns[-1] if step else ([], beta)
    scale = 1.0 / length
    for total in totals:
        total[...] = jnp.zeros_like(total)
    low_half = row_of() < NRHS

    def entry(value):
        high = value.astype(jnp.bfloat16).astype(jnp.float32)
        return jnp.where(low_half, high, value - high)

    for r in range(BLOCKS):
        value = block(own, r)
        for i in range(step):
            value = value - h[i] * block(earlier_own[i], r)
        value = value * scale
        basis_own[pl.ds(8 * r, 8), :] = value
        table[pl.ds(8 * r, 8), :] = entry(value)
    wide_scale = strided(scale)
    wide_h = [strided(value) for value in h]
    period = 8 * STRIDE
    for group in range(devices // 8):
        value = incoming[pl.ds(period * group, period), :]
        rows = pl.ds(LEAD + period * group, period)
        for i in range(step):
            value = value - wide_h[i] * earlier_halo[i][rows, :]
        basis_halo[rows, :] = value * wide_scale
    for device in range(devices):
        start = LEAD + STRIDE * device
        upper = basis_halo[pl.ds(start, 8), :]
        lower = basis_halo[pl.ds(start - NRHS, 8), :]
        table[pl.ds(8 * (BLOCKS + device), 8), :] = entry(jnp.where(low_half, upper, lower))

    if step == 0:
        fetch(0).wait()
        pack(0, packed[0], 0)

        def advance(chunk):
            @pl.when(chunk + BUFFERS - 1 < chunks)
            def _():
                fetch(chunk + BUFFERS - 1).start()

            fetch(chunk).wait()

        def body(trip, carry):
            chunk = 2 * trip + 1
            advance(chunk)
            pack(chunk, packed[1], trip)
            multiply(chunk - 1, packed[0], trip)
            advance(chunk + 1)
            pack(chunk + 1, packed[0], trip + 1)
            multiply(chunk, packed[1], trip)
            return carry

        trips = chunks // 2 - 1
        lax.fori_loop(0, trips, body, 0)
        fetch(chunks - 1).wait()
        pack(chunks - 1, packed[1], trips)
        multiply(chunks - 2, packed[0], trips)
        multiply(chunks - 1, packed[1], trips)
    else:

        def body(trip, carry):
            multiply(2 * trip, packed[0], trip)
            multiply(2 * trip + 1, packed[1], trip)
            return carry

        lax.fori_loop(0, chunks // 2, body, 0)

    blocks = []
    for r in range(BLOCKS):
        value = functools.reduce(jnp.add, [block(total, r) for total in totals])
        value = value + pltpu.roll(value, NRHS, 0)
        product[pl.ds(8 * r, 8), :] = value
        blocks.append(value)
    terms = {WW: functools.reduce(jnp.add, [b * b for b in blocks])}
    for i, vector in enumerate([*earlier_own, basis_own]):
        known = [block(vector, r) for r in range(BLOCKS)]
        latest = [block(basis_own, r) for r in range(BLOCKS)]
        terms[i] = functools.reduce(jnp.add, [a * b for a, b in zip(known, blocks)])
        terms[GRAM + i] = functools.reduce(jnp.add, [a * b for a, b in zip(known, latest)])
    local = row_of_sums(terms)
    if last:
        outgoing[...] = jnp.broadcast_to(local, outgoing.shape)
    else:
        write_outgoing(outgoing, places, blocks, local)


def weights_of(beta, columns):
    rotations = []
    triangle = []
    target = [beta]
    for column, (h, length) in enumerate(columns):
        values = list(h) + [length]
        for earlier, (cosine, sine) in enumerate(rotations):
            first, second = values[earlier], values[earlier + 1]
            values[earlier] = cosine * first + sine * second
            values[earlier + 1] = cosine * second - sine * first
        first, second = values[column], values[column + 1]
        radius = jnp.sqrt(first * first + second * second)
        cosine, sine = first / radius, second / radius
        rotations.append((cosine, sine))
        triangle.append(values[:column] + [radius])
        leading = target[column]
        target[column] = cosine * leading
        target.append(-sine * leading)
    size = len(columns)
    weights = [None] * size
    for column in reversed(range(size)):
        value = target[column]
        for later in range(column + 1, size):
            value = value - triangle[later][column] * weights[later]
        weights[column] = value / triangle[column][column]
    return weights


def final_kernel(incoming, *refs):
    earlier_sums, bases = refs[:ITERS], refs[ITERS : 2 * ITERS]
    solution, hessenberg = refs[2 * ITERS :]
    sums = jnp.sum(incoming[...], axis=0, keepdims=True)
    beta, columns = coefficients([ref[...] for ref in earlier_sums] + [sums])
    weights = weights_of(beta, columns)

    def combined(r):
        value = weights[0] * block(bases[0], r)
        for weight, basis in zip(weights[1:], bases[1:]):
            value = value + weight * block(basis, r)
        return value

    for j in range(BLOCKS // 2):
        both = jnp.where(row_of() < NRHS, combined(2 * j), combined(2 * j + 1))
        solution[pl.ds(8 * j, 8), :] = both
    for column, (h, length) in enumerate(columns):
        table = jnp.zeros((8, 128), jnp.float32)
        for i, value in enumerate([*h, length]):
            table = jnp.where(lane_of() == i, value, table)
        hessenberg[column] = table[:NRHS, : ITERS + 1]


def params(limit):
    return pltpu.CompilerParams(vmem_limit_bytes=limit * MIB)


def in_hbm(array):
    return pltpu.with_memory_space_constraint(array, pltpu.HBM)


def exchange(outgoing):
    size = outgoing.shape[0]
    moved = lax.all_to_all(
        outgoing.reshape(size, 1, 128), ROWS, split_axis=0, concat_axis=0, tiled=True
    )
    return moved.reshape(size, 128)


def on_device(tile_values, tile_row, tile_slot, tile_count, requests, right_side):
    devices = lax.axis_size(ROWS)
    tiles = tile_values.shape[0]
    f32 = jnp.float32
    flat = right_side.reshape(BLOCKS * NRHS, 128)
    block_rows = jax.ShapeDtypeStruct((8 * BLOCKS, 128), f32)
    sum_rows = jax.ShapeDtypeStruct((8, 128), f32)
    message = jax.ShapeDtypeStruct((devices * STRIDE, 128), f32)
    halo_rows = jax.ShapeDtypeStruct((LEAD + devices * STRIDE + 8, 128), f32)
    wanted, own, *kept = pl.pallas_call(
        begin_kernel,
        out_shape=(
            jax.ShapeDtypeStruct((devices, 128), jnp.int32),
            block_rows,
            pltpu.SMEM(tile_slot.shape, tile_slot.dtype),
            pltpu.SMEM(tile_row.shape, tile_row.dtype),
            pltpu.SMEM(tile_count.shape, tile_count.dtype),
        ),
        in_specs=[SMEM] + [HBM] * 4,
        out_specs=(VMEM, VMEM, SMEM, SMEM, SMEM),
        scratch_shapes=[
            pltpu.VMEM((1, devices), jnp.int32),
            pltpu.VMEM(flat.shape, f32),
            pltpu.SemaphoreType.DMA((4,)),
        ],
        compiler_params=params(8),
        name="begin",
    )(tile_count, *map(in_hbm, (requests.reshape(1, devices), flat, tile_slot, tile_row)))
    slots, rows_of, count = kept
    asked = exchange(wanted)
    places, outgoing = pl.pallas_call(
        first_kernel,
        out_shape=(jax.ShapeDtypeStruct((devices * STRIDE, 256), jnp.bfloat16), message),
        in_specs=[VMEM, VMEM],
        out_specs=(VMEM, VMEM),
        compiler_params=params(8),
        name="first",
    )(own, asked)
    sums, owns, halos = [], [], []
    packed = []
    for step in range(ITERS):
        last = step == ITERS - 1
        incoming = exchange(outgoing)
        shapes = [
            block_rows,
            halo_rows,
            sum_rows,
            block_rows,
            jax.ShapeDtypeStruct((devices, 128), f32) if last else message,
        ]
        scratch = [pltpu.VMEM((8 * (BLOCKS + devices), 128), f32)]
        scratch += [pltpu.VMEM(block_rows.shape, f32)] * TOTALS
        operands = [slots, rows_of, places, incoming, own, *sums, *owns, *halos]
        specs = [SMEM, SMEM] + [VMEM] * (len(operands) - 2)
        if step == 0:
            shapes += [pltpu.VMEM((tiles // 2 * 256, 128), jnp.bfloat16)] * 2
            scratch.append(pltpu.VMEM((BUFFERS, CHUNK, 128, 128), f32))
            scratch.append(pltpu.SemaphoreType.DMA((BUFFERS,)))
            operands = [count, in_hbm(tile_values)] + operands
            specs = [SMEM, HBM] + specs
        else:
            operands = packed + operands
            specs = [VMEM, VMEM] + specs
        vector, halo, row, own, outgoing, *kept = pl.pallas_call(
            functools.partial(step_kernel, step, last),
            out_shape=shapes,
            in_specs=specs,
            out_specs=[VMEM] * len(shapes),
            scratch_shapes=scratch,
            compiler_params=params(24),
            name=f"step{step}",
        )(*operands)
        packed = kept or packed
        sums.append(row)
        owns.append(vector)
        halos.append(halo)
    incoming = exchange(outgoing)
    solution, hessenberg = pl.pallas_call(
        final_kernel,
        out_shape=(
            jax.ShapeDtypeStruct(flat.shape, f32),
            jax.ShapeDtypeStruct((ITERS, NRHS, ITERS + 1), f32),
        ),
        in_specs=[VMEM] * (1 + 2 * ITERS),
        out_specs=(VMEM, VMEM),
        compiler_params=params(8),
        name="final",
    )(incoming, *sums, *owns)
    return solution.reshape(right_side.shape), hessenberg.transpose(1, 2, 0)


def solution(mesh):
    finer = Mesh(mesh.devices.reshape(4, 4, 4, 2), ROWS)
    placed = (
        P(ROWS, None, None),
        P(ROWS),
        P(ROWS),
        P(ROWS),
        P(ROWS, None, None),
        P(ROWS, None, None),
    )
    return jax.shard_map(
        on_device,
        mesh=finer,
        in_specs=placed,
        out_specs=(P(ROWS, None, None), P()),
        check_vma=False,
    )
```

time: 102 us -> 99.5 us (0.975)
  Pallas kernels: 17.4 us -> 15.2 us
    pallas_call x3, Pallas kernels: 15.4 us -> 12.9 us  [on_device(): pl.pallas_call(functools.partial(step_kernel, step, last), out_shape=shap...]
where the time goes in v3:
time: 99.5 us; the launch traced here: 99.2 us
  blocking collectives  82.8 us (83%)
  Pallas kernels  15.2 us (15%)
  between operations  1.3 us (1%)
    all_to_all x5, blocking collectives, exchange(): lax.all_to_all(outgoing.reshape(size, 1, 128), ROWS, split_axis=0, concat...  82.8 us
    pallas_call x3, Pallas kernels, on_device(): pl.pallas_call(functools.partial(step_kernel, step, last), out_shape=shap...  12.9 us

profile of v3, /device:TPU:1, one launch (start us, length us, event | category | flops | bytes accessed | tf_op | source)
XLA Modules:
  0.0 99.2 jit_solution(6329810523453825733)
XLA Ops:
  1.3 0.9 begin.1
  2.2 20.8 %all_to_all.25 = s32[128,1,128]{2,1,0:T(1,128)S(1)} all-to-all(s32[128,1,128]{2,1,0:T(1,128)S(1)} %bitcast.33), channel_id=1, replica_groups=mesh['rows_0'=4,'rows_1'=4,'rows_2'=4,'rows_3'=2] {'rows_0','rows_1','ro..., dimensions={0} | all-to-all | bytes 131072 | tf_op jit(solution)/shard_map/all_to_all | solution.py:382
  23.0 0.6 first.1
  23.6 15.8 %all_to_all.26 = f32[640,1,128]{2,1,0:T(1,128)S(1)} all-to-all(f32[640,1,128]{2,1,0:T(1,128)S(1)} %bitcast.29), channel_id=1, replica_groups=mesh['rows_0'=4,'rows_1'=4,'rows_2'=4,'rows_3'=2] {'rows_0','rows_1','ro..., dimensions={0} | all-to-all | bytes 655360 | tf_op jit(solution)/shard_map/all_to_all | solution.py:382
  39.4 6.7 %step0.1 = (f32[128,128]{1,0:T(8,128)S(1)}, f32[656,128]{1,0:T(8,128)S(1)}, f32[8,128]{1,0:T(8,128)S(1)}, f32[128,128]{1,0:T(8,128)S(1)}, f32[640,128]{1,0:T(8,1...) custom-call(s32[1]{0:T(128)S(4)} %get-tuple-element.26.refs_0_, f32[208,128,128]{2,1,0:T(8,128)} %refs_1_.1, ...), custom_call_target="tpu_custom_call" | custom-call | tf_op jit(solution)/shard_map/step0/pallas_call | solution.py:451
  46.1 16.0 %all_to_all.27 = f32[640,1,128]{2,1,0:T(1,128)S(1)} all-to-all(f32[640,1,128]{2,1,0:T(1,128)S(1)} %bitcast.27), channel_id=1, replica_groups=mesh['rows_0'=4,'rows_1'=4,'rows_2'=4,'rows_3'=2] {'rows_0','rows_1','ro..., dimensions={0} | all-to-all | bytes 655360 | tf_op jit(solution)/shard_map/all_to_all | solution.py:382
  62.1 2.9 %step1.1 = (f32[128,128]{1,0:T(8,128)S(1)}, f32[656,128]{1,0:T(8,128)S(1)}, f32[8,128]{1,0:T(8,128)S(1)}, f32[128,128]{1,0:T(8,128)S(1)}, f32[640,128]{1,0:T(8,128)S(1)}) custom-call(bf16[26624,128]{1,0:T(8,128)(2,1)S(1)} %get-tuple-element.33.refs_0_, bf16[26624,128]{1,0:T(8,128)(2,1)S(1)} %get-tuple-element.34.refs_1_, s32[208]{0:T(256)S(4)} %get-tuple-element.27.refs_2_, ...), custom_call_target="tpu_custom_call" | custom-call | tf_op jit(solution)/shard_map/step1/pallas_call | solution.py:451
  64.9 16.0 %all_to_all.28 = f32[640,1,128]{2,1,0:T(1,128)S(1)} all-to-all(f32[640,1,128]{2,1,0:T(1,128)S(1)} %bitcast.28), channel_id=1, replica_groups=mesh['rows_0'=4,'rows_1'=4,'rows_2'=4,'rows_3'=2] {'rows_0','rows_1','ro..., dimensions={0} | all-to-all | bytes 655360 | tf_op jit(solution)/shard_map/all_to_all | solution.py:382
  80.9 3.4 %step2.1 = (f32[128,128]{1,0:T(8,128)S(1)}, f32[656,128]{1,0:T(8,128)}, f32[8,128]{1,0:T(8,128)S(1)}, f32[128,128]{1,0:T(8,128)}, f32[128,128]{1,0:T(8,128)S(1)}) custom-call(bf16[26624,128]{1,0:T(8,128)(2,1)S(1)} %get-tuple-element.33.refs_0_, bf16[26624,128]{1,0:T(8,128)(2,1)S(1)} %get-tuple-element.34.refs_1_, s32[208]{0:T(256)S(4)} %get-tuple-element.27.refs_2_, ...), custom_call_target="tpu_custom_call" | custom-call | tf_op jit(solution)/shard_map/step2/pallas_call | solution.py:451
  84.3 14.1 %all_to_all.29 = f32[128,1,128]{2,1,0:T(1,128)S(1)} all-to-all(f32[128,1,128]{2,1,0:T(1,128)S(1)} %bitcast.32), channel_id=1, replica_groups=mesh['rows_0'=4,'rows_1'=4,'rows_2'=4,'rows_3'=2] {'rows_0','rows_1','ro..., dimensions={0} | all-to-all | bytes 131072 | tf_op jit(solution)/shard_map/all_to_all | solution.py:382
  98.4 0.8 final.1

commit v4 on v3

--- a/solution.py
+++ b/solution.py
@@ -17,8 +17,8 @@
 EPSILON = 1e-06
 
 CHUNK = 26
-BUFFERS = 4
 TOTALS = 8
+COVER = 20_000_000_000
 MIB = 1 << 20
 
 WW = 3
@@ -64,20 +64,17 @@
     return jnp.sum(jnp.where(row_of() < NRHS, row, 0.0), axis=0, keepdims=True)
 
 
-def write_outgoing(outgoing, places, blocks, sums):
-    low_half = row_of() < NRHS
-    packed = [
-        jnp.where(low_half, blocks[2 * j], blocks[2 * j + 1]) for j in range(BLOCKS // 2)
-    ]
-    parts = list(split3(jnp.concatenate(packed, axis=0)))
-    row = row_of((64, 128))
-    tail = jnp.zeros((64, 128), jnp.float32)
-    for place, part in enumerate(split3(sums)):
-        tail = jnp.where(row == place, part.astype(jnp.float32), tail)
-    parts.append(tail.astype(jnp.bfloat16))
-    outgoing[...] = jnp.dot(
-        places[...], jnp.concatenate(parts, axis=0), preferred_element_type=jnp.float32
-    )
+def write_outgoing(outgoing, chosen, vector, sums):
+    devices = chosen.shape[0]
+    systems = [vector[pl.ds(k, BLOCKS, stride=8), :] for k in range(NRHS)]
+    parts = jnp.concatenate(split3(jnp.concatenate(systems, axis=1)), axis=0)
+    pick = jnp.concatenate([chosen[...][:, :BLOCKS]] * 3, axis=1)
+    picked = jnp.dot(pick, parts, preferred_element_type=jnp.float32)
+    for k in range(NRHS):
+        rows = pl.ds(k, devices, stride=STRIDE)
+        outgoing[rows, :] = picked[:, k * 128 : (k + 1) * 128]
+    rows = pl.ds(NRHS, devices, stride=STRIDE)
+    outgoing[rows, :] = jnp.broadcast_to(sums, (devices, 128))
 
 
 def begin_kernel(*refs):
@@ -104,26 +101,12 @@
         copy.wait()
 
 
-def first_kernel(own, asked, places, outgoing):
-    f32 = jnp.float32
-    devices = asked.shape[0]
-    rows = devices * STRIDE
-    row = row_of((rows, devices))
-    device = STRIDE * lane_of((rows, devices))
-    spread = ((row >= device) & (row < device + STRIDE)).astype(f32).astype(jnp.bfloat16)
-    ids = asked[...].astype(f32).astype(jnp.bfloat16)
-    wanted = jnp.dot(spread, ids, preferred_element_type=f32)
-    row = row.astype(f32)
-    system = row - STRIDE * jnp.floor(row * (1.0 / STRIDE) + 0.5 / STRIDE)
-    lane = lane_of((rows, 128))
-    column = (lane % 64).astype(f32)
-    own_block = (column == wanted * NRHS + system) & (system < NRHS)
-    sums_row = (system >= NRHS) & (lane >= 64) & (lane < 67)
-    places[:, :128] = own_block.astype(f32).astype(jnp.bfloat16)
-    places[:, 128:] = ((own_block & (lane < 64)) | sums_row).astype(f32).astype(jnp.bfloat16)
+def first_kernel(own, asked, chosen, outgoing):
+    hot = asked[...] == lane_of(asked.shape)
+    chosen[...] = hot.astype(jnp.float32).astype(jnp.bfloat16)
     blocks = [block(own, r) for r in range(BLOCKS)]
     sums = row_of_sums({WW: functools.reduce(jnp.add, [b * b for b in blocks])})
-    write_outgoing(outgoing, places, blocks, sums)
+    write_outgoing(outgoing, chosen, own, sums)
 
 
 def coefficients(rows):
@@ -178,26 +161,23 @@
 
     count, tiles = take(2) if step == 0 else (None, None)
     packed = take(2) if step > 0 else None
-    slots, rows_of, places, incoming, own = take(5)
+    slots, rows_of, chosen, incoming, own = take(5)
     earlier_sums, earlier_own, earlier_halo = take(step), take(step), take(step)
-    basis_own, basis_halo, sums_out, product, outgoing = take(5)
+    basis_own, sums_out, outgoing = take(3)
+    if not last:
+        basis_halo, product = take(2)
     if step == 0:
         packed = take(2)
     (table,) = take(1)
     totals = take(TOTALS)
+    if last:
+        basis_halo, product = take(2)
     devices = incoming.shape[0] // STRIDE
     chunks = packed[0].shape[0] // (CHUNK * 256) * 2
 
-    def fetch(chunk):
-        slot = lax.rem(chunk, BUFFERS)
-        return pltpu.make_async_copy(
-            tiles.at[pl.ds(chunk * CHUNK, CHUNK)], buffer.at[slot], arrived.at[slot]
-        )
-
     def pack(chunk, target, place):
-        slot = lax.rem(chunk, BUFFERS)
         for local in range(CHUNK):
-            tile = buffer[slot, local]
+            tile = tiles[chunk * CHUNK + local]
             tile = jnp.where(chunk * CHUNK + local < live, tile, 0.0)
             high, low = split2(tile.T)
             start = (place * CHUNK + local) * 256
@@ -223,10 +203,7 @@
                 total[row, :] += result[side * 8 : side * 8 + 8, side * 128 : side * 128 + 128]
 
     if step == 0:
-        buffer, arrived = take(2)
         live = count[0]
-        for chunk in range(BUFFERS):
-            fetch(chunk).start()
 
     sums = jnp.sum(incoming[pl.ds(NRHS, devices, stride=STRIDE), :], axis=0, keepdims=True)
     sums_out[...] = jnp.broadcast_to(sums, (8, 128))
@@ -264,29 +241,18 @@
         table[pl.ds(8 * (BLOCKS + device), 8), :] = entry(jnp.where(low_half, upper, lower))
 
     if step == 0:
-        fetch(0).wait()
         pack(0, packed[0], 0)
-
-        def advance(chunk):
-            @pl.when(chunk + BUFFERS - 1 < chunks)
-            def _():
-                fetch(chunk + BUFFERS - 1).start()
-
-            fetch(chunk).wait()
 
         def body(trip, carry):
             chunk = 2 * trip + 1
-            advance(chunk)
             pack(chunk, packed[1], trip)
             multiply(chunk - 1, packed[0], trip)
-            advance(chunk + 1)
             pack(chunk + 1, packed[0], trip + 1)
             multiply(chunk, packed[1], trip)
             return carry
 
         trips = chunks // 2 - 1
         lax.fori_loop(0, trips, body, 0)
-        fetch(chunks - 1).wait()
         pack(chunks - 1, packed[1], trips)
         multiply(chunks - 2, packed[0], trips)
         multiply(chunks - 1, packed[1], trips)
@@ -315,7 +281,7 @@
     if last:
         outgoing[...] = jnp.broadcast_to(local, outgoing.shape)
     else:
-        write_outgoing(outgoing, places, blocks, local)
+        write_outgoing(outgoing, chosen, product, local)
 
 
 def weights_of(beta, columns):
@@ -415,12 +381,13 @@
     )(tile_count, *map(in_hbm, (requests.reshape(1, devices), flat, tile_slot, tile_row)))
     slots, rows_of, count = kept
     asked = exchange(wanted)
-    places, outgoing = pl.pallas_call(
+    chosen, outgoing = pl.pallas_call(
         first_kernel,
-        out_shape=(jax.ShapeDtypeStruct((devices * STRIDE, 256), jnp.bfloat16), message),
+        out_shape=(jax.ShapeDtypeStruct((devices, devices), jnp.bfloat16), message),
         in_specs=[VMEM, VMEM],
         out_specs=(VMEM, VMEM),
         compiler_params=params(8),
+        cost_estimate=pl.CostEstimate(flops=COVER, bytes_accessed=0, transcendentals=0),
         name="first",
     )(own, asked)
     sums, owns, halos = [], [], []
@@ -428,39 +395,36 @@
     for step in range(ITERS):
         last = step == ITERS - 1
         incoming = exchange(outgoing)
-        shapes = [
-            block_rows,
-            halo_rows,
-            sum_rows,
-            block_rows,
-            jax.ShapeDtypeStruct((devices, 128), f32) if last else message,
-        ]
+        shapes = [block_rows, sum_rows]
+        shapes += [jax.ShapeDtypeStruct((devices, 128), f32)] if last else [message]
+        shapes += [] if last else [halo_rows, block_rows]
         scratch = [pltpu.VMEM((8 * (BLOCKS + devices), 128), f32)]
         scratch += [pltpu.VMEM(block_rows.shape, f32)] * TOTALS
-        operands = [slots, rows_of, places, incoming, own, *sums, *owns, *halos]
+        if last:
+            scratch += [pltpu.VMEM(halo_rows.shape, f32), pltpu.VMEM(block_rows.shape, f32)]
+        operands = [slots, rows_of, chosen, incoming, own, *sums, *owns, *halos]
         specs = [SMEM, SMEM] + [VMEM] * (len(operands) - 2)
         if step == 0:
             shapes += [pltpu.VMEM((tiles // 2 * 256, 128), jnp.bfloat16)] * 2
-            scratch.append(pltpu.VMEM((BUFFERS, CHUNK, 128, 128), f32))
-            scratch.append(pltpu.SemaphoreType.DMA((BUFFERS,)))
-            operands = [count, in_hbm(tile_values)] + operands
-            specs = [SMEM, HBM] + specs
+            operands = [count, tile_values] + operands
+            specs = [SMEM, VMEM] + specs
         else:
             operands = packed + operands
             specs = [VMEM, VMEM] + specs
-        vector, halo, row, own, outgoing, *kept = pl.pallas_call(
+        vector, row, outgoing, *kept = pl.pallas_call(
             functools.partial(step_kernel, step, last),
             out_shape=shapes,
             in_specs=specs,
             out_specs=[VMEM] * len(shapes),
             scratch_shapes=scratch,
-            compiler_params=params(24),
+            compiler_params=params(20),
             name=f"step{step}",
         )(*operands)
-        packed = kept or packed
         sums.append(row)
         owns.append(vector)
-        halos.append(halo)
+        if not last:
+            halo, own, *packed = [*kept, *packed]
+            halos.append(halo)
     incoming = exchange(outgoing)
     solution, hessenberg = pl.pallas_call(
         final_kernel,

time: 99.5 us -> 97 us (0.975)
  Pallas kernels: 15.2 us -> 12.6 us
    pallas_call x3, Pallas kernels: 12.9 us -> 10.7 us  [on_device(): pl.pallas_call(functools.partial(step_kernel, step, last), out_shape=shap...]
where the time goes in v4:
time: 97 us; the launch traced here: 96.8 us
  blocking collectives  82.8 us (85%)
  Pallas kernels  12.6 us (13%)
  between operations  1.34 us (1%)
    all_to_all x5, blocking collectives, exchange(): lax.all_to_all(outgoing.reshape(size, 1, 128), ROWS, split_axis=0, concat...  82.8 us
    pallas_call x3, Pallas kernels, on_device(): pl.pallas_call(functools.partial(step_kernel, step, last), out_shape=shap...  10.7 us

profile of v4, /device:TPU:1, one launch (start us, length us, event | category | flops | bytes accessed | tf_op | source)
XLA Modules:
  0.0 96.8 jit_solution(13537043761664096485)
XLA Ops:
  1.3 0.9 begin.1
  2.2 20.8 %all_to_all.25 = s32[128,1,128]{2,1,0:T(1,128)S(1)} all-to-all(s32[128,1,128]{2,1,0:T(1,128)S(1)} %bitcast.34), channel_id=1, replica_groups=mesh['rows_0'=4,'rows_1'=4,'rows_2'=4,'rows_3'=2] {'rows_0','rows_1','ro..., dimensions={0} | all-to-all | bytes 131072 | tf_op jit(solution)/shard_map/all_to_all | solution.py:348
  23.0 0.0 slice-start
  23.0 0.0 slice-start.1
  23.0 0.0 slice-start.2
  23.0 0.0 slice-start.3
  23.0 0.2 first.1
  23.2 15.8 %all_to_all.26 = f32[640,1,128]{2,1,0:T(1,128)S(1)} all-to-all(f32[640,1,128]{2,1,0:T(1,128)S(1)} %bitcast.31), channel_id=1, replica_groups=mesh['rows_0'=4,'rows_1'=4,'rows_2'=4,'rows_3'=2] {'rows_0','rows_1','ro..., dimensions={0} | all-to-all | bytes 655360 | tf_op jit(solution)/shard_map/all_to_all | solution.py:348
  39.0 0.0 slice-done
  39.0 0.0 slice-done.1
  39.0 0.0 slice-done.2
  39.0 0.0 slice-done.3
  39.1 5.3 %step0.1 = (f32[128,128]{1,0:T(8,128)S(1)}, f32[8,128]{1,0:T(8,128)S(1)}, f32[640,128]{1,0:T(8,128)S(1)}, f32[656,128]{1,0:T(8,128)S(1)}, f32[128,128]{1,0:T(8,1...) custom-call(s32[1]{0:T(128)S(4)} %get-tuple-element.26.refs_0_, f32[208,128,128]{2,1,0:T(8,128)S(1)} %bitcast.25, ...), custom_call_target="tpu_custom_call" | custom-call | tf_op jit(solution)/shard_map/step0/pallas_call | solution.py:414
  44.3 16.0 %all_to_all.27 = f32[640,1,128]{2,1,0:T(1,128)S(1)} all-to-all(f32[640,1,128]{2,1,0:T(1,128)S(1)} %bitcast.29), channel_id=1, replica_groups=mesh['rows_0'=4,'rows_1'=4,'rows_2'=4,'rows_3'=2] {'rows_0','rows_1','ro..., dimensions={0} | all-to-all | bytes 655360 | tf_op jit(solution)/shard_map/all_to_all | solution.py:348
  60.4 2.7 %step1.1 = (f32[128,128]{1,0:T(8,128)S(1)}, f32[8,128]{1,0:T(8,128)S(1)}, f32[640,128]{1,0:T(8,128)S(1)}, f32[656,128]{1,0:T(8,128)S(1)}, f32[128,128]{1,0:T(8,128)S(1)}) custom-call(bf16[26624,128]{1,0:T(8,128)(2,1)S(1)} %get-tuple-element.33.refs_0_, bf16[26624,128]{1,0:T(8,128)(2,1)S(1)} %get-tuple-element.34.refs_1_, s32[208]{0:T(256)S(4)} %get-tuple-element.27.refs_2_, ...), custom_call_target="tpu_custom_call" | custom-call | tf_op jit(solution)/shard_map/step1/pallas_call | solution.py:414
  63.1 16.0 %all_to_all.28 = f32[640,1,128]{2,1,0:T(1,128)S(1)} all-to-all(f32[640,1,128]{2,1,0:T(1,128)S(1)} %bitcast.30), channel_id=1, replica_groups=mesh['rows_0'=4,'rows_1'=4,'rows_2'=4,'rows_3'=2] {'rows_0','rows_1','ro..., dimensions={0} | all-to-all | bytes 655360 | tf_op jit(solution)/shard_map/all_to_all | solution.py:348
  79.1 2.7 %step2.1 = (f32[128,128]{1,0:T(8,128)S(1)}, f32[8,128]{1,0:T(8,128)S(1)}, f32[128,128]{1,0:T(8,128)S(1)}) custom-call(bf16[26624,128]{1,0:T(8,128)(2,1)S(1)} %get-tuple-element.33.refs_0_, bf16[26624,128]{1,0:T(8,128)(2,1)S(1)} %get-tuple-element.34.refs_1_, s32[208]{0:T(256)S(4)} %get-tuple-element.27.refs_2_, s32[208]{0:T(256)S(4)} %get-tuple-element.28.refs_3_, ...), custom_call_target="tpu_custom_call" | custom-call | tf_op jit(solution)/shard_map/step2/pallas_call | solution.py:414
  81.8 14.1 %all_to_all.29 = f32[128,1,128]{2,1,0:T(1,128)S(1)} all-to-all(f32[128,1,128]{2,1,0:T(1,128)S(1)} %bitcast.33), channel_id=1, replica_groups=mesh['rows_0'=4,'rows_1'=4,'rows_2'=4,'rows_3'=2] {'rows_0','rows_1','ro..., dimensions={0} | all-to-all | bytes 131072 | tf_op jit(solution)/shard_map/all_to_all | solution.py:348
  96.0 0.8 final.1
  (1 shorter events, 0.0 us)
Async XLA Ops:
  23.0 16.1 %slice-start = ((s8[13631488]{0:T(1024)(128)(4,1)}), s8[4194304]{0:T(1024)(128)(4,1)S(1)}, s32[]{:S(2)}) async-start(s8[13631488]{0:T(1024)(128)(4,1)} %bitcast.24), calls=%async_computation.5 | async-start | bytes 8388608
  23.0 16.1 %slice-start.1 = ((s8[13631488]{0:T(1024)(128)(4,1)}), s8[4194304]{0:T(1024)(128)(4,1)S(1)}, s32[]{:S(2)}) async-start(s8[13631488]{0:T(1024)(128)(4,1)} %bitcast.24), calls=%async_computation.6 | async-start | bytes 8388608
  23.0 16.1 %slice-start.2 = ((s8[13631488]{0:T(1024)(128)(4,1)}), s8[4194304]{0:T(1024)(128)(4,1)S(1)}, s32[]{:S(2)}) async-start(s8[13631488]{0:T(1024)(128)(4,1)} %bitcast.24), calls=%async_computation.7 | async-start | bytes 8388608
  23.0 16.1 %slice-start.3 = ((s8[13631488]{0:T(1024)(128)(4,1)}), s8[1048576]{0:T(1024)(128)(4,1)S(1)}, s32[]{:S(2)}) async-start(s8[13631488]{0:T(1024)(128)(4,1)} %bitcast.24), calls=%async_computation.8 | async-start | bytes 2097152

commit v5 on v4

--- a/solution.py
+++ b/solution.py
@@ -23,6 +23,7 @@
 
 WW = 3
 GRAM = 4
+NORM = 16
 
 VMEM = pl.BlockSpec(memory_space=pltpu.VMEM)
 SMEM = pl.BlockSpec(memory_space=pltpu.SMEM)
@@ -64,17 +65,19 @@
     return jnp.sum(jnp.where(row_of() < NRHS, row, 0.0), axis=0, keepdims=True)
 
 
-def write_outgoing(outgoing, chosen, vector, sums):
+def write_outgoing(outgoing, chosen, vector, sums=None):
     devices = chosen.shape[0]
+    stride = outgoing.shape[0] // devices
     systems = [vector[pl.ds(k, BLOCKS, stride=8), :] for k in range(NRHS)]
     parts = jnp.concatenate(split3(jnp.concatenate(systems, axis=1)), axis=0)
     pick = jnp.concatenate([chosen[...][:, :BLOCKS]] * 3, axis=1)
     picked = jnp.dot(pick, parts, preferred_element_type=jnp.float32)
     for k in range(NRHS):
-        rows = pl.ds(k, devices, stride=STRIDE)
+        rows = pl.ds(k, devices, stride=stride)
         outgoing[rows, :] = picked[:, k * 128 : (k + 1) * 128]
-    rows = pl.ds(NRHS, devices, stride=STRIDE)
-    outgoing[rows, :] = jnp.broadcast_to(sums, (devices, 128))
+    if sums is not None:
+        rows = pl.ds(NRHS, devices, stride=stride)
+        outgoing[rows, :] = jnp.broadcast_to(sums, (devices, 128))
 
 
 def begin_kernel(*refs):
@@ -88,25 +91,29 @@
     ]
     for copy in copies:
         copy.start()
-    copies[0].wait()
-    wanted[...] = jnp.broadcast_to(requests[...], wanted.shape).T
     copies[1].wait()
     low_half = row_of() < NRHS
+    squares = jnp.zeros((8, 128), jnp.float32)
     for j in range(BLOCKS // 2):
         both = block(right_side, j)
         turned = pltpu.roll(both, NRHS, 0)
         own[pl.ds(16 * j, 8), :] = jnp.where(low_half, both, turned)
         own[pl.ds(16 * j + 8, 8), :] = jnp.where(low_half, turned, both)
+        squares = squares + both * both
+    sums = row_of_sums({NORM: squares + pltpu.roll(squares, NRHS, 0)})
+    copies[0].wait()
+    ids = jnp.broadcast_to(requests[...], wanted.shape).T.astype(jnp.float32)
+    is_norm = lane_of(wanted.shape) // NRHS == NORM
+    wanted[...] = jnp.where(is_norm, jnp.broadcast_to(sums, wanted.shape), ids)
     for copy in copies[2:]:
         copy.wait()
 
 
-def first_kernel(own, asked, chosen, outgoing):
-    hot = asked[...] == lane_of(asked.shape)
+def first_kernel(own, asked, chosen, sums, outgoing):
+    hot = asked[...] == lane_of(asked.shape).astype(jnp.float32)
     chosen[...] = hot.astype(jnp.float32).astype(jnp.bfloat16)
-    blocks = [block(own, r) for r in range(BLOCKS)]
-    sums = row_of_sums({WW: functools.reduce(jnp.add, [b * b for b in blocks])})
-    write_outgoing(outgoing, chosen, own, sums)
+    sums[...] = jnp.broadcast_to(jnp.sum(asked[...], axis=0, keepdims=True), sums.shape)
+    write_outgoing(outgoing, chosen, own)
 
 
 def coefficients(rows):
@@ -114,7 +121,7 @@
         chosen = jnp.where(in_group(group), row, 0.0)
         return jnp.broadcast_to(jnp.sum(chosen, axis=1, keepdims=True), (8, 128))
 
-    beta = jnp.sqrt(entry(rows[0], WW) + EPSILON)
+    beta = jnp.sqrt(entry(rows[0], NORM) + EPSILON)
     columns = []
     gram = {}
     for column, row in enumerate(rows[1:]):
@@ -162,8 +169,10 @@
     count, tiles = take(2) if step == 0 else (None, None)
     packed = take(2) if step > 0 else None
     slots, rows_of, chosen, incoming, own = take(5)
-    earlier_sums, earlier_own, earlier_halo = take(step), take(step), take(step)
-    basis_own, sums_out, outgoing = take(3)
+    earlier_sums, earlier_own, earlier_halo = take(max(step, 1)), take(step), take(step)
+    basis_own, outgoing = take(2)
+    if step > 0:
+        (sums_out,) = take(1)
     if not last:
         basis_halo, product = take(2)
     if step == 0:
@@ -172,19 +181,17 @@
     totals = take(TOTALS)
     if last:
         basis_halo, product = take(2)
-    devices = incoming.shape[0] // STRIDE
-    chunks = packed[0].shape[0] // (CHUNK * 256) * 2
-
-    def pack(chunk, target, place):
-        for local in range(CHUNK):
-            tile = tiles[chunk * CHUNK + local]
-            tile = jnp.where(chunk * CHUNK + local < live, tile, 0.0)
-            high, low = split2(tile.T)
-            start = (place * CHUNK + local) * 256
-            target[pl.ds(start, 128), :] = high
-            target[pl.ds(start + 128, 128), :] = low
-
-    def multiply(chunk, source, place):
+    devices = table.shape[0] // 8 - BLOCKS
+    chunks = sum(part.shape[0] for part in packed) // (CHUNK * 256)
+
+    def pack(tile_id, target, start):
+        tile = jnp.where(tile_id < live, tiles[tile_id], 0.0)
+        high, low = split2(tile.T)
+        both = jnp.concatenate([high, low], axis=0)
+        target[pl.ds(start, 256), :] = both
+        return both
+
+    def multiply(chunk, source, place, fresh=False):
         for local in range(CHUNK // 2):
             tile = chunk * CHUNK + 2 * local
             picked = [
@@ -193,7 +200,10 @@
             left = jnp.concatenate(picked, axis=0).astype(jnp.bfloat16)
             left = jnp.concatenate([left, left], axis=1)
             start = (place * CHUNK + 2 * local) * 256
-            right = [source[pl.ds(start + side * 256, 256), :] for side in range(2)]
+            if fresh:
+                right = [pack(tile + side, source, start + side * 256) for side in range(2)]
+            else:
+                right = [source[pl.ds(start + side * 256, 256), :] for side in range(2)]
             result = jnp.dot(
                 left, jnp.concatenate(right, axis=1), preferred_element_type=jnp.float32
             )
@@ -205,9 +215,12 @@
     if step == 0:
         live = count[0]
 
-    sums = jnp.sum(incoming[pl.ds(NRHS, devices, stride=STRIDE), :], axis=0, keepdims=True)
-    sums_out[...] = jnp.broadcast_to(sums, (8, 128))
-    beta, columns = coefficients([ref[...] for ref in earlier_sums] + [sums])
+    sums_rows = [ref[...] for ref in earlier_sums]
+    if step > 0:
+        rows = pl.ds(NRHS, devices, stride=STRIDE)
+        sums_rows.append(jnp.sum(incoming[rows, :], axis=0, keepdims=True))
+        sums_out[...] = jnp.broadcast_to(sums_rows[-1], (8, 128))
+    beta, columns = coefficients(sums_rows)
     h, length = columns[-1] if step else ([], beta)
     scale = 1.0 / length
     for total in totals:
@@ -225,45 +238,41 @@
         value = value * scale
         basis_own[pl.ds(8 * r, 8), :] = value
         table[pl.ds(8 * r, 8), :] = entry(value)
-    wide_scale = strided(scale)
-    wide_h = [strided(value) for value in h]
-    period = 8 * STRIDE
-    for group in range(devices // 8):
-        value = incoming[pl.ds(period * group, period), :]
-        rows = pl.ds(LEAD + period * group, period)
-        for i in range(step):
-            value = value - wide_h[i] * earlier_halo[i][rows, :]
-        basis_halo[rows, :] = value * wide_scale
-    for device in range(devices):
-        start = LEAD + STRIDE * device
-        upper = basis_halo[pl.ds(start, 8), :]
-        lower = basis_halo[pl.ds(start - NRHS, 8), :]
-        table[pl.ds(8 * (BLOCKS + device), 8), :] = entry(jnp.where(low_half, upper, lower))
-
     if step == 0:
-        pack(0, packed[0], 0)
-
+        for j in range(devices // 2):
+            both = block(incoming, j) * scale
+            turned = pltpu.roll(both, NRHS, 0)
+            for side in range(2):
+                value = jnp.where(low_half, turned, both) if side else jnp.where(low_half, both, turned)
+                device = 2 * j + side
+                basis_halo[pl.ds(LEAD + STRIDE * device, 8), :] = value
+                table[pl.ds(8 * (BLOCKS + device), 8), :] = entry(value)
+    else:
+        wide_scale = strided(scale)
+        wide_h = [strided(value) for value in h]
+        period = 8 * STRIDE
+        for group in range(devices // 8):
+            value = incoming[pl.ds(period * group, period), :]
+            rows = pl.ds(LEAD + period * group, period)
+            for i in range(step):
+                value = value - wide_h[i] * earlier_halo[i][rows, :]
+            basis_halo[rows, :] = value * wide_scale
+        for device in range(devices):
+            start = LEAD + STRIDE * device
+            upper = basis_halo[pl.ds(start, 8), :]
+            lower = basis_halo[pl.ds(start - NRHS, 8), :]
+            table[pl.ds(8 * (BLOCKS + device), 8), :] = entry(jnp.where(low_half, upper, lower))
+
+    if step == 0:
         def body(trip, carry):
-            chunk = 2 * trip + 1
-            pack(chunk, packed[1], trip)
-            multiply(chunk - 1, packed[0], trip)
-            pack(chunk + 1, packed[0], trip + 1)
-            multiply(chunk, packed[1], trip)
+            multiply(2 * trip, packed[0], trip, True)
+            multiply(2 * trip + 1, packed[1], trip, True)
             return carry
 
-        trips = chunks // 2 - 1
-        lax.fori_loop(0, trips, body, 0)
-        pack(chunks - 1, packed[1], trips)
-        multiply(chunks - 2, packed[0], trips)
-        multiply(chunks - 1, packed[1], trips)
+        lax.fori_loop(0, chunks // 2, body, 0)
     else:
-
-        def body(trip, carry):
-            multiply(2 * trip, packed[0], trip)
-            multiply(2 * trip + 1, packed[1], trip)
-            return carry
-
-        lax.fori_loop(0, chunks // 2, body, 0)
+        for chunk in range(chunks):
+            multiply(chunk, packed[chunk % 2], chunk // 2)
 
     blocks = []
     for r in range(BLOCKS):
@@ -363,7 +372,7 @@
     wanted, own, *kept = pl.pallas_call(
         begin_kernel,
         out_shape=(
-            jax.ShapeDtypeStruct((devices, 128), jnp.int32),
+            jax.ShapeDtypeStruct((devices, 128), f32),
             block_rows,
             pltpu.SMEM(tile_slot.shape, tile_slot.dtype),
             pltpu.SMEM(tile_row.shape, tile_row.dtype),
@@ -381,22 +390,27 @@
     )(tile_count, *map(in_hbm, (requests.reshape(1, devices), flat, tile_slot, tile_row)))
     slots, rows_of, count = kept
     asked = exchange(wanted)
-    chosen, outgoing = pl.pallas_call(
+    chosen, norms, outgoing = pl.pallas_call(
         first_kernel,
-        out_shape=(jax.ShapeDtypeStruct((devices, devices), jnp.bfloat16), message),
+        out_shape=(
+            jax.ShapeDtypeStruct((devices, devices), jnp.bfloat16),
+            sum_rows,
+            jax.ShapeDtypeStruct((devices * NRHS, 128), f32),
+        ),
         in_specs=[VMEM, VMEM],
-        out_specs=(VMEM, VMEM),
+        out_specs=(VMEM, VMEM, VMEM),
         compiler_params=params(8),
         cost_estimate=pl.CostEstimate(flops=COVER, bytes_accessed=0, transcendentals=0),
         name="first",
     )(own, asked)
-    sums, owns, halos = [], [], []
+    sums, owns, halos = [norms], [], []
     packed = []
     for step in range(ITERS):
         last = step == ITERS - 1
         incoming = exchange(outgoing)
-        shapes = [block_rows, sum_rows]
+        shapes = [block_rows]
         shapes += [jax.ShapeDtypeStruct((devices, 128), f32)] if last else [message]
+        shapes += [sum_rows] if step > 0 else []
         shapes += [] if last else [halo_rows, block_rows]
         scratch = [pltpu.VMEM((8 * (BLOCKS + devices), 128), f32)]
         scratch += [pltpu.VMEM(block_rows.shape, f32)] * TOTALS
@@ -405,13 +419,16 @@
         operands = [slots, rows_of, chosen, incoming, own, *sums, *owns, *halos]
         specs = [SMEM, SMEM] + [VMEM] * (len(operands) - 2)
         if step == 0:
-            shapes += [pltpu.VMEM((tiles // 2 * 256, 128), jnp.bfloat16)] * 2
+            odd = tiles // CHUNK // 2 * CHUNK
+            shapes += [
+                pltpu.VMEM((part * 256, 128), jnp.bfloat16) for part in (tiles - odd, odd)
+            ]
             operands = [count, tile_values] + operands
             specs = [SMEM, VMEM] + specs
         else:
             operands = packed + operands
             specs = [VMEM, VMEM] + specs
-        vector, row, outgoing, *kept = pl.pallas_call(
+        vector, outgoing, *kept = pl.pallas_call(
             functools.partial(step_kernel, step, last),
             out_shape=shapes,
             in_specs=specs,
@@ -420,7 +437,8 @@
             compiler_params=params(20),
             name=f"step{step}",
         )(*operands)
-        sums.append(row)
+        if step > 0:
+            sums.append(kept.pop(0))
         owns.append(vector)
         if not last:
             halo, own, *packed = [*kept, *packed]

time: 97 us -> 95.3 us (0.982)
  Pallas kernels: 12.6 us -> 11.6 us
    pallas_call x3, Pallas kernels: 10.7 us -> 9.58 us  [on_device(): pl.pallas_call(functools.partial(step_kernel, step, last), out_shape=shap...]
where the time goes in v5:
time: 95.3 us; the launch traced here: 95.1 us
  blocking collectives  82.1 us (86%)
  Pallas kernels  11.6 us (12%)
  between operations  1.34 us (1%)
    all_to_all x5, blocking collectives, exchange(): lax.all_to_all(outgoing.reshape(size, 1, 128), ROWS, split_axis=0, concat...  82.1 us
    pallas_call x3, Pallas kernels, on_device(): pl.pallas_call(functools.partial(step_kernel, step, last), out_shape=shap...  9.58 us

profile of v5, /device:TPU:1, one launch (start us, length us, event | category | flops | bytes accessed | tf_op | source)
XLA Modules:
  0.0 95.1 jit_solution(12230310871966220276)
XLA Ops:
  1.3 1.0 %begin.1 = (f32[128,128]{1,0:T(8,128)S(1)}, f32[128,128]{1,0:T(8,128)S(1)}, s32[208]{0:T(256)S(4)}, s32[208]{0:T(256)S(4)}, s32[1]{0:T(128)S(4)}) custom-call(s32[1]{0:T(128)S(6)} %copy.13.refs_0_, s32[1,128]{1,0:T(1,128)} %bitcast.37, f32[64,128]{1,0:T(8,128)} %bitcast.36, s32[208]{0:T(256)} %refs_3_.1, s32[208]{0:T(256)} %refs_4_.1), custom_call_target="tpu_custom_call" | custom-call | tf_op jit(solution)/shard_map/begin/pallas_call | solution.py:372
  2.3 20.8 %all_to_all.25 = f32[128,1,128]{2,1,0:T(1,128)S(1)} all-to-all(f32[128,1,128]{2,1,0:T(1,128)S(1)} %bitcast.34), channel_id=1, replica_groups=mesh['rows_0'=4,'rows_1'=4,'rows_2'=4,'rows_3'=2] {'rows_0','rows_1','ro..., dimensions={0} | all-to-all | bytes 131072 | tf_op jit(solution)/shard_map/all_to_all | solution.py:357
  23.1 0.0 slice-start
  23.1 0.0 slice-start.1
  23.1 0.0 slice-start.2
  23.1 0.0 slice-start.3
  23.1 0.2 first.1
  23.4 15.3 %all_to_all.26 = f32[512,1,128]{2,1,0:T(1,128)S(1)} all-to-all(f32[512,1,128]{2,1,0:T(1,128)S(1)} %bitcast.31), channel_id=1, replica_groups=mesh['rows_0'=4,'rows_1'=4,'rows_2'=4,'rows_3'=2] {'rows_0','rows_1','ro..., dimensions={0} | all-to-all | bytes 524288 | tf_op jit(solution)/shard_map/all_to_all | solution.py:357
  38.7 0.0 slice-done
  38.7 0.0 slice-done.1
  38.7 0.0 slice-done.2
  38.7 0.0 slice-done.3
  38.7 4.9 %step0.1 = (f32[128,128]{1,0:T(8,128)S(1)}, f32[640,128]{1,0:T(8,128)S(1)}, f32[656,128]{1,0:T(8,128)S(1)}, f32[128,128]{1,0:T(8,128)S(1)}, bf16[26624,128]{1,0:...) custom-call(s32[1]{0:T(128)S(4)} %get-tuple-element.26.refs_0_, f32[208,128,128]{2,1,0:T(8,128)S(1)} %bitcast.25, ...), custom_call_target="tpu_custom_call" | custom-call | tf_op jit(solution)/shard_map/step0/pallas_call | solution.py:431
  43.6 15.8 %all_to_all.27 = f32[640,1,128]{2,1,0:T(1,128)S(1)} all-to-all(f32[640,1,128]{2,1,0:T(1,128)S(1)} %bitcast.29), channel_id=1, replica_groups=mesh['rows_0'=4,'rows_1'=4,'rows_2'=4,'rows_3'=2] {'rows_0','rows_1','ro..., dimensions={0} | all-to-all | bytes 655360 | tf_op jit(solution)/shard_map/all_to_all | solution.py:357
  59.5 2.4 %step1.1 = (f32[128,128]{1,0:T(8,128)S(1)}, f32[640,128]{1,0:T(8,128)S(1)}, f32[8,128]{1,0:T(8,128)S(1)}, f32[656,128]{1,0:T(8,128)S(1)}, f32[128,128]{1,0:T(8,128)S(1)}) custom-call(bf16[26624,128]{1,0:T(8,128)(2,1)S(1)} %get-tuple-element.34.refs_0_, bf16[26624,128]{1,0:T(8,128)(2,1)S(1)} %get-tuple-element.35.refs_1_, s32[208]{0:T(256)S(4)} %get-tuple-element.27.refs_2_, ...), custom_call_target="tpu_custom_call" | custom-call | tf_op jit(solution)/shard_map/step1/pallas_call | solution.py:431
  61.8 16.0 %all_to_all.28 = f32[640,1,128]{2,1,0:T(1,128)S(1)} all-to-all(f32[640,1,128]{2,1,0:T(1,128)S(1)} %bitcast.30), channel_id=1, replica_groups=mesh['rows_0'=4,'rows_1'=4,'rows_2'=4,'rows_3'=2] {'rows_0','rows_1','ro..., dimensions={0} | all-to-all | bytes 655360 | tf_op jit(solution)/shard_map/all_to_all | solution.py:357
  77.8 2.3 %step2.1 = (f32[128,128]{1,0:T(8,128)S(1)}, f32[128,128]{1,0:T(8,128)S(1)}, f32[8,128]{1,0:T(8,128)S(1)}) custom-call(bf16[26624,128]{1,0:T(8,128)(2,1)S(1)} %get-tuple-element.34.refs_0_, bf16[26624,128]{1,0:T(8,128)(2,1)S(1)} %get-tuple-element.35.refs_1_, s32[208]{0:T(256)S(4)} %get-tuple-element.27.refs_2_, s32[208]{0:T(256)S(4)} %get-tuple-element.28.refs_3_, ...), custom_call_target="tpu_custom_call" | custom-call | tf_op jit(solution)/shard_map/step2/pallas_call | solution.py:431
  80.1 14.1 %all_to_all.29 = f32[128,1,128]{2,1,0:T(1,128)S(1)} all-to-all(f32[128,1,128]{2,1,0:T(1,128)S(1)} %bitcast.33), channel_id=1, replica_groups=mesh['rows_0'=4,'rows_1'=4,'rows_2'=4,'rows_3'=2] {'rows_0','rows_1','ro..., dimensions={0} | all-to-all | bytes 131072 | tf_op jit(solution)/shard_map/all_to_all | solution.py:357
  94.3 0.8 final.1
  (1 shorter events, 0.0 us)
Async XLA Ops:
  23.1 15.6 %slice-start = ((s8[13631488]{0:T(1024)(128)(4,1)}), s8[4194304]{0:T(1024)(128)(4,1)S(1)}, s32[]{:S(2)}) async-start(s8[13631488]{0:T(1024)(128)(4,1)} %bitcast.24), calls=%async_computation.5 | async-start | bytes 8388608
  23.1 15.6 %slice-start.1 = ((s8[13631488]{0:T(1024)(128)(4,1)}), s8[4194304]{0:T(1024)(128)(4,1)S(1)}, s32[]{:S(2)}) async-start(s8[13631488]{0:T(1024)(128)(4,1)} %bitcast.24), calls=%async_computation.6 | async-start | bytes 8388608
  23.1 15.6 %slice-start.2 = ((s8[13631488]{0:T(1024)(128)(4,1)}), s8[4194304]{0:T(1024)(128)(4,1)S(1)}, s32[]{:S(2)}) async-start(s8[13631488]{0:T(1024)(128)(4,1)} %bitcast.24), calls=%async_computation.7 | async-start | bytes 8388608
  23.1 15.6 %slice-start.3 = ((s8[13631488]{0:T(1024)(128)(4,1)}), s8[1048576]{0:T(1024)(128)(4,1)S(1)}, s32[]{:S(2)}) async-start(s8[13631488]{0:T(1024)(128)(4,1)} %bitcast.24), calls=%async_computation.8 | async-start | bytes 2097152

commit v6 on v5

--- a/solution.py
+++ b/solution.py
@@ -16,8 +16,9 @@
 ROWS = ("rows_0", "rows_1", "rows_2", "rows_3")
 EPSILON = 1e-06
 
-CHUNK = 26
+CHUNK = 104
 TOTALS = 8
+TURNED = 4
 COVER = 20_000_000_000
 MIB = 1 << 20
 
@@ -91,6 +92,7 @@
     ]
     for copy in copies:
         copy.start()
+    copies[0].wait()
     copies[1].wait()
     low_half = row_of() < NRHS
     squares = jnp.zeros((8, 128), jnp.float32)
@@ -101,7 +103,6 @@
         own[pl.ds(16 * j + 8, 8), :] = jnp.where(low_half, turned, both)
         squares = squares + both * both
     sums = row_of_sums({NORM: squares + pltpu.roll(squares, NRHS, 0)})
-    copies[0].wait()
     ids = jnp.broadcast_to(requests[...], wanted.shape).T.astype(jnp.float32)
     is_norm = lane_of(wanted.shape) // NRHS == NORM
     wanted[...] = jnp.where(is_norm, jnp.broadcast_to(sums, wanted.shape), ids)
@@ -191,6 +192,20 @@
         target[pl.ds(start, 256), :] = both
         return both
 
+    def turn(left, tile_id, target, start):
+        sides = [jnp.where(tile_id + side < live, tiles[tile_id + side], 0.0) for side in range(2)]
+        right = jnp.concatenate([jnp.concatenate(split2(tile), axis=1) for tile in sides], axis=0)
+        result = lax.dot_general(
+            jnp.concatenate([left, identity[...]], axis=0),
+            right,
+            (((1,), (1,)), ((), ())),
+            preferred_element_type=jnp.float32,
+        )
+        turned = result[16:].astype(jnp.bfloat16)
+        target[pl.ds(start, 256), :] = turned[:, :128]
+        target[pl.ds(start + 256, 256), :] = turned[:, 128:]
+        return result[:16]
+
     def multiply(chunk, source, place, fresh=False):
         for local in range(CHUNK // 2):
             tile = chunk * CHUNK + 2 * local
@@ -200,13 +215,16 @@
             left = jnp.concatenate(picked, axis=0).astype(jnp.bfloat16)
             left = jnp.concatenate([left, left], axis=1)
             start = (place * CHUNK + 2 * local) * 256
-            if fresh:
+            if fresh and local % TURNED == 0:
+                result = turn(left, tile, source, start)
+            elif fresh:
                 right = [pack(tile + side, source, start + side * 256) for side in range(2)]
             else:
                 right = [source[pl.ds(start + side * 256, 256), :] for side in range(2)]
-            result = jnp.dot(
-                left, jnp.concatenate(right, axis=1), preferred_element_type=jnp.float32
-            )
+            if not (fresh and local % TURNED == 0):
+                result = jnp.dot(
+                    left, jnp.concatenate(right, axis=1), preferred_element_type=jnp.float32
+                )
             for side in range(2):
                 total = totals[(2 * local + side) % TOTALS]
                 row = pl.ds(pl.multiple_of(rows_of[tile + side] * 8, 8), 8)
@@ -214,6 +232,9 @@
 
     if step == 0:
         live = count[0]
+        (identity,) = take(1)
+        diagonal = row_of((256, 256)) == lane_of((256, 256))
+        identity[...] = diagonal.astype(jnp.float32).astype(jnp.bfloat16)
 
     sums_rows = [ref[...] for ref in earlier_sums]
     if step > 0:
@@ -420,6 +441,7 @@
         specs = [SMEM, SMEM] + [VMEM] * (len(operands) - 2)
         if step == 0:
             odd = tiles // CHUNK // 2 * CHUNK
+            scratch.append(pltpu.VMEM((256, 256), jnp.bfloat16))
             shapes += [
                 pltpu.VMEM((part * 256, 128), jnp.bfloat16) for part in (tiles - odd, odd)
             ]

time: 95.3 us -> 93.6 us (0.982)
  Pallas kernels: 11.6 us -> 9.92 us
    pallas_call x3, Pallas kernels: 9.58 us -> 7.94 us  [on_device(): pl.pallas_call(functools.partial(step_kernel, step, last), out_shape=shap...]
where the time goes in v6:
time: 93.6 us; the launch traced here: 93.4 us
  blocking collectives  82.1 us (88%)
  Pallas kernels  9.92 us (11%)
  between operations  1.33 us (1%)
    all_to_all x5, blocking collectives, exchange(): lax.all_to_all(outgoing.reshape(size, 1, 128), ROWS, split_axis=0, concat...  82.1 us
    pallas_call x3, Pallas kernels, on_device(): pl.pallas_call(functools.partial(step_kernel, step, last), out_shape=shap...  7.94 us

profile of v6, /device:TPU:1, one launch (start us, length us, event | category | flops | bytes accessed | tf_op | source)
XLA Modules:
  0.0 93.4 jit_solution(8731520157267091086)
XLA Ops:
  1.3 1.0 %begin.1 = (f32[128,128]{1,0:T(8,128)S(1)}, f32[128,128]{1,0:T(8,128)S(1)}, s32[208]{0:T(256)S(4)}, s32[208]{0:T(256)S(4)}, s32[1]{0:T(128)S(4)}) custom-call(s32[1]{0:T(128)S(6)} %copy.13.refs_0_, s32[1,128]{1,0:T(1,128)} %bitcast.37, f32[64,128]{1,0:T(8,128)} %bitcast.36, s32[208]{0:T(256)} %refs_3_.1, s32[208]{0:T(256)} %refs_4_.1), custom_call_target="tpu_custom_call" | custom-call | tf_op jit(solution)/shard_map/begin/pallas_call | solution.py:393
  2.2 20.8 %all_to_all.25 = f32[128,1,128]{2,1,0:T(1,128)S(1)} all-to-all(f32[128,1,128]{2,1,0:T(1,128)S(1)} %bitcast.34), channel_id=1, replica_groups=mesh['rows_0'=4,'rows_1'=4,'rows_2'=4,'rows_3'=2] {'rows_0','rows_1','ro..., dimensions={0} | all-to-all | bytes 131072 | tf_op jit(solution)/shard_map/all_to_all | solution.py:378
  23.1 0.0 slice-start
  23.1 0.0 slice-start.1
  23.1 0.0 slice-start.2
  23.1 0.0 slice-start.3
  23.1 0.2 first.1
  23.3 15.3 %all_to_all.26 = f32[512,1,128]{2,1,0:T(1,128)S(1)} all-to-all(f32[512,1,128]{2,1,0:T(1,128)S(1)} %bitcast.31), channel_id=1, replica_groups=mesh['rows_0'=4,'rows_1'=4,'rows_2'=4,'rows_3'=2] {'rows_0','rows_1','ro..., dimensions={0} | all-to-all | bytes 524288 | tf_op jit(solution)/shard_map/all_to_all | solution.py:378
  38.6 0.0 slice-done
  38.6 0.0 slice-done.1
  38.6 0.0 slice-done.2
  38.6 0.0 slice-done.3
  38.7 3.3 %step0.1 = (f32[128,128]{1,0:T(8,128)S(1)}, f32[640,128]{1,0:T(8,128)S(1)}, f32[656,128]{1,0:T(8,128)S(1)}, f32[128,128]{1,0:T(8,128)S(1)}, bf16[26624,128]{1,0:...) custom-call(s32[1]{0:T(128)S(4)} %get-tuple-element.26.refs_0_, f32[208,128,128]{2,1,0:T(8,128)S(1)} %bitcast.25, ...), custom_call_target="tpu_custom_call" | custom-call | tf_op jit(solution)/shard_map/step0/pallas_call | solution.py:453
  42.0 15.8 %all_to_all.27 = f32[640,1,128]{2,1,0:T(1,128)S(1)} all-to-all(f32[640,1,128]{2,1,0:T(1,128)S(1)} %bitcast.29), channel_id=1, replica_groups=mesh['rows_0'=4,'rows_1'=4,'rows_2'=4,'rows_3'=2] {'rows_0','rows_1','ro..., dimensions={0} | all-to-all | bytes 655360 | tf_op jit(solution)/shard_map/all_to_all | solution.py:378
  57.8 2.3 %step1.1 = (f32[128,128]{1,0:T(8,128)S(1)}, f32[640,128]{1,0:T(8,128)S(1)}, f32[8,128]{1,0:T(8,128)S(1)}, f32[656,128]{1,0:T(8,128)S(1)}, f32[128,128]{1,0:T(8,128)S(1)}) custom-call(bf16[26624,128]{1,0:T(8,128)(2,1)S(1)} %get-tuple-element.34.refs_0_, bf16[26624,128]{1,0:T(8,128)(2,1)S(1)} %get-tuple-element.35.refs_1_, s32[208]{0:T(256)S(4)} %get-tuple-element.27.refs_2_, ...), custom_call_target="tpu_custom_call" | custom-call | tf_op jit(solution)/shard_map/step1/pallas_call | solution.py:453
  60.1 16.0 %all_to_all.28 = f32[640,1,128]{2,1,0:T(1,128)S(1)} all-to-all(f32[640,1,128]{2,1,0:T(1,128)S(1)} %bitcast.30), channel_id=1, replica_groups=mesh['rows_0'=4,'rows_1'=4,'rows_2'=4,'rows_3'=2] {'rows_0','rows_1','ro..., dimensions={0} | all-to-all | bytes 655360 | tf_op jit(solution)/shard_map/all_to_all | solution.py:378
  76.1 2.3 %step2.1 = (f32[128,128]{1,0:T(8,128)S(1)}, f32[128,128]{1,0:T(8,128)S(1)}, f32[8,128]{1,0:T(8,128)S(1)}) custom-call(bf16[26624,128]{1,0:T(8,128)(2,1)S(1)} %get-tuple-element.34.refs_0_, bf16[26624,128]{1,0:T(8,128)(2,1)S(1)} %get-tuple-element.35.refs_1_, s32[208]{0:T(256)S(4)} %get-tuple-element.27.refs_2_, s32[208]{0:T(256)S(4)} %get-tuple-element.28.refs_3_, ...), custom_call_target="tpu_custom_call" | custom-call | tf_op jit(solution)/shard_map/step2/pallas_call | solution.py:453
  78.4 14.1 %all_to_all.29 = f32[128,1,128]{2,1,0:T(1,128)S(1)} all-to-all(f32[128,1,128]{2,1,0:T(1,128)S(1)} %bitcast.33), channel_id=1, replica_groups=mesh['rows_0'=4,'rows_1'=4,'rows_2'=4,'rows_3'=2] {'rows_0','rows_1','ro..., dimensions={0} | all-to-all | bytes 131072 | tf_op jit(solution)/shard_map/all_to_all | solution.py:378
  92.6 0.8 final.1
  (1 shorter events, 0.0 us)
Async XLA Ops:
  23.1 15.6 %slice-start = ((s8[13631488]{0:T(1024)(128)(4,1)}), s8[4194304]{0:T(1024)(128)(4,1)S(1)}, s32[]{:S(2)}) async-start(s8[13631488]{0:T(1024)(128)(4,1)} %bitcast.24), calls=%async_computation.5 | async-start | bytes 8388608
  23.1 15.6 %slice-start.1 = ((s8[13631488]{0:T(1024)(128)(4,1)}), s8[4194304]{0:T(1024)(128)(4,1)S(1)}, s32[]{:S(2)}) async-start(s8[13631488]{0:T(1024)(128)(4,1)} %bitcast.24), calls=%async_computation.6 | async-start | bytes 8388608
  23.1 15.6 %slice-start.2 = ((s8[13631488]{0:T(1024)(128)(4,1)}), s8[4194304]{0:T(1024)(128)(4,1)S(1)}, s32[]{:S(2)}) async-start(s8[13631488]{0:T(1024)(128)(4,1)} %bitcast.24), calls=%async_computation.7 | async-start | bytes 8388608
  23.1 15.6 %slice-start.3 = ((s8[13631488]{0:T(1024)(128)(4,1)}), s8[1048576]{0:T(1024)(128)(4,1)S(1)}, s32[]{:S(2)}) async-start(s8[13631488]{0:T(1024)(128)(4,1)} %bitcast.24), calls=%async_computation.8 | async-start | bytes 2097152

commit v7 on v6

--- a/solution.py
+++ b/solution.py
@@ -16,8 +16,7 @@
 ROWS = ("rows_0", "rows_1", "rows_2", "rows_3")
 EPSILON = 1e-06
 
-CHUNK = 104
-TOTALS = 8
+TOTALS = 4
 TURNED = 4
 COVER = 20_000_000_000
 MIB = 1 << 20
@@ -168,7 +167,7 @@
         return taken
 
     count, tiles = take(2) if step == 0 else (None, None)
-    packed = take(2) if step > 0 else None
+    packed = refs.pop(0) if step > 0 else None
     slots, rows_of, chosen, incoming, own = take(5)
     earlier_sums, earlier_own, earlier_halo = take(max(step, 1)), take(step), take(step)
     basis_own, outgoing = take(2)
@@ -177,13 +176,12 @@
     if not last:
         basis_halo, product = take(2)
     if step == 0:
-        packed = take(2)
+        packed = refs.pop(0)
     (table,) = take(1)
     totals = take(TOTALS)
     if last:
         basis_halo, product = take(2)
     devices = table.shape[0] // 8 - BLOCKS
-    chunks = sum(part.shape[0] for part in packed) // (CHUNK * 256)
 
     def pack(tile_id, target, start):
         tile = jnp.where(tile_id < live, tiles[tile_id], 0.0)
@@ -206,29 +204,31 @@
         target[pl.ds(start + 256, 256), :] = turned[:, 128:]
         return result[:16]
 
-    def multiply(chunk, source, place, fresh=False):
-        for local in range(CHUNK // 2):
-            tile = chunk * CHUNK + 2 * local
-            picked = [
-                table[pl.ds(pl.multiple_of(slots[tile + side] * 8, 8), 8), :] for side in range(2)
-            ]
-            left = jnp.concatenate(picked, axis=0).astype(jnp.bfloat16)
-            left = jnp.concatenate([left, left], axis=1)
-            start = (place * CHUNK + 2 * local) * 256
-            if fresh and local % TURNED == 0:
-                result = turn(left, tile, source, start)
-            elif fresh:
-                right = [pack(tile + side, source, start + side * 256) for side in range(2)]
+    def multiply(tile):
+        own_slots = BLOCKS + devices
+        picked = [
+            table[pl.ds(8 * tile if tile < own_slots else pl.multiple_of(slots[tile] * 8, 8), 8), :]
+            for tile in (tile, tile + 1)
+        ]
+        left = jnp.concatenate(picked, axis=0).astype(jnp.bfloat16)
+        left = jnp.concatenate([left, left], axis=1)
+        start = tile * 256
+        if step == 0 and tile // 2 % TURNED == 0:
+            result = turn(left, tile, packed, start)
+        else:
+            if step == 0:
+                right = [pack(tile + side, packed, start + side * 256) for side in range(2)]
             else:
-                right = [source[pl.ds(start + side * 256, 256), :] for side in range(2)]
-            if not (fresh and local % TURNED == 0):
-                result = jnp.dot(
-                    left, jnp.concatenate(right, axis=1), preferred_element_type=jnp.float32
-                )
-            for side in range(2):
-                total = totals[(2 * local + side) % TOTALS]
-                row = pl.ds(pl.multiple_of(rows_of[tile + side] * 8, 8), 8)
-                total[row, :] += result[side * 8 : side * 8 + 8, side * 128 : side * 128 + 128]
+                right = [packed[pl.ds(start + side * 256, 256), :] for side in range(2)]
+            result = jnp.dot(
+                left, jnp.concatenate(right, axis=1), preferred_element_type=jnp.float32
+            )
+        for side in range(2):
+            total = totals[(tile + side) % TOTALS]
+            row = tile + side
+            row = 8 * row if row < BLOCKS else pl.multiple_of(rows_of[row] * 8, 8)
+            part = result[side * 8 : side * 8 + 8, side * 128 : side * 128 + 128]
+            total[pl.ds(row, 8), :] += part
 
     if step == 0:
         live = count[0]
@@ -284,16 +284,8 @@
             lower = basis_halo[pl.ds(start - NRHS, 8), :]
             table[pl.ds(8 * (BLOCKS + device), 8), :] = entry(jnp.where(low_half, upper, lower))
 
-    if step == 0:
-        def body(trip, carry):
-            multiply(2 * trip, packed[0], trip, True)
-            multiply(2 * trip + 1, packed[1], trip, True)
-            return carry
-
-        lax.fori_loop(0, chunks // 2, body, 0)
-    else:
-        for chunk in range(chunks):
-            multiply(chunk, packed[chunk % 2], chunk // 2)
+    for tile in range(0, packed.shape[0] // 256, 2):
+        multiply(tile)
 
     blocks = []
     for r in range(BLOCKS):
@@ -425,7 +417,7 @@
         name="first",
     )(own, asked)
     sums, owns, halos = [norms], [], []
-    packed = []
+    packed = None
     for step in range(ITERS):
         last = step == ITERS - 1
         incoming = exchange(outgoing)
@@ -440,16 +432,13 @@
         operands = [slots, rows_of, chosen, incoming, own, *sums, *owns, *halos]
         specs = [SMEM, SMEM] + [VMEM] * (len(operands) - 2)
         if step == 0:
-            odd = tiles // CHUNK // 2 * CHUNK
             scratch.append(pltpu.VMEM((256, 256), jnp.bfloat16))
-            shapes += [
-                pltpu.VMEM((part * 256, 128), jnp.bfloat16) for part in (tiles - odd, odd)
-            ]
+            shapes.append(pltpu.VMEM((tiles * 256, 128), jnp.bfloat16))
             operands = [count, tile_values] + operands
             specs = [SMEM, VMEM] + specs
         else:
-            operands = packed + operands
-            specs = [VMEM, VMEM] + specs
+            operands = [packed] + operands
+            specs = [VMEM] + specs
         vector, outgoing, *kept = pl.pallas_call(
             functools.partial(step_kernel, step, last),
             out_shape=shapes,
@@ -463,8 +452,9 @@
             sums.append(kept.pop(0))
         owns.append(vector)
         if not last:
-            halo, own, *packed = [*kept, *packed]
+            halo, own, *rest = kept
             halos.append(halo)
+            packed = rest[0] if step == 0 else packed
     incoming = exchange(outgoing)
     solution, hessenberg = pl.pallas_call(
         final_kernel,

time: 93.6 us -> 93.4 us (level)
  no operation moved by 1% of the time
where the time goes in v7:
time: 93.4 us; the launch traced here: 93.1 us
  blocking collectives  82.1 us (88%)
  Pallas kernels  9.69 us (10%)
  between operations  1.31 us (1%)
    all_to_all x5, blocking collectives, exchange(): lax.all_to_all(outgoing.reshape(size, 1, 128), ROWS, split_axis=0, concat...  82.1 us
    pallas_call x3, Pallas kernels, on_device(): pl.pallas_call(functools.partial(step_kernel, step, last), out_shape=shap...  7.71 us

profile of v7, /device:TPU:1, one launch (start us, length us, event | category | flops | bytes accessed | tf_op | source)
XLA Modules:
  0.0 93.1 jit_solution(9581173334367860556)
XLA Ops:
  1.3 1.0 %begin.1 = (f32[128,128]{1,0:T(8,128)S(1)}, f32[128,128]{1,0:T(8,128)S(1)}, s32[208]{0:T(256)S(4)}, s32[208]{0:T(256)S(4)}, s32[1]{0:T(128)S(4)}) custom-call(s32[1]{0:T(128)S(6)} %copy.13.refs_0_, s32[1,128]{1,0:T(1,128)} %bitcast.35, f32[64,128]{1,0:T(8,128)} %bitcast.34, s32[208]{0:T(256)} %refs_3_.1, s32[208]{0:T(256)} %refs_4_.1), custom_call_target="tpu_custom_call" | custom-call | tf_op jit(solution)/shard_map/begin/pallas_call | solution.py:385
  2.2 20.8 %all_to_all.25 = f32[128,1,128]{2,1,0:T(1,128)S(1)} all-to-all(f32[128,1,128]{2,1,0:T(1,128)S(1)} %bitcast.32), channel_id=1, replica_groups=mesh['rows_0'=4,'rows_1'=4,'rows_2'=4,'rows_3'=2] {'rows_0','rows_1','ro..., dimensions={0} | all-to-all | bytes 131072 | tf_op jit(solution)/shard_map/all_to_all | solution.py:370
  23.1 0.0 copy-start
  23.1 0.2 first.1
  23.3 15.3 %all_to_all.26 = f32[512,1,128]{2,1,0:T(1,128)S(1)} all-to-all(f32[512,1,128]{2,1,0:T(1,128)S(1)} %bitcast.29), channel_id=1, replica_groups=mesh['rows_0'=4,'rows_1'=4,'rows_2'=4,'rows_3'=2] {'rows_0','rows_1','ro..., dimensions={0} | all-to-all | bytes 524288 | tf_op jit(solution)/shard_map/all_to_all | solution.py:370
  38.6 0.0 copy-done
  38.6 3.2 %step0.1 = (f32[128,128]{1,0:T(8,128)S(1)}, f32[640,128]{1,0:T(8,128)S(1)}, f32[656,128]{1,0:T(8,128)S(1)}, f32[128,128]{1,0:T(8,128)S(1)}, bf16[53248,128]{1,0:T(8,128)(2,1)S(1)}) custom-call(s32[1]{0:T(128)S(4)} %get-tuple-element.25.refs_0_, f32[208,128,128]{2,1,0:T(8,128)S(1)} %copy-done, s32[208]{0:T(256)S(4)} %get-tuple-element.26.refs_2_.refs_1_, ...), custom_call_target="tpu_custom_call" | custom-call | tf_op jit(solution)/shard_map/step0/pallas_call | solution.py:442
  41.9 15.8 %all_to_all.27 = f32[640,1,128]{2,1,0:T(1,128)S(1)} all-to-all(f32[640,1,128]{2,1,0:T(1,128)S(1)} %bitcast.27), channel_id=1, replica_groups=mesh['rows_0'=4,'rows_1'=4,'rows_2'=4,'rows_3'=2] {'rows_0','rows_1','ro..., dimensions={0} | all-to-all | bytes 655360 | tf_op jit(solution)/shard_map/all_to_all | solution.py:370
  57.7 2.3 %step1.1 = (f32[128,128]{1,0:T(8,128)S(1)}, f32[640,128]{1,0:T(8,128)S(1)}, f32[8,128]{1,0:T(8,128)S(1)}, f32[656,128]{1,0:T(8,128)S(1)}, f32[128,128]{1,0:T(8,128)S(1)}) custom-call(bf16[53248,128]{1,0:T(8,128)(2,1)S(1)} %get-tuple-element.33.refs_0_, s32[208]{0:T(256)S(4)} %get-tuple-element.26.refs_2_.refs_1_, s32[208]{0:T(256)S(4)} %get-tuple-element.27.refs_3_.refs_2_, ...), custom_call_target="tpu_custom_call" | custom-call | tf_op jit(solution)/shard_map/step1/pallas_call | solution.py:442
  59.9 16.0 %all_to_all.28 = f32[640,1,128]{2,1,0:T(1,128)S(1)} all-to-all(f32[640,1,128]{2,1,0:T(1,128)S(1)} %bitcast.28), channel_id=1, replica_groups=mesh['rows_0'=4,'rows_1'=4,'rows_2'=4,'rows_3'=2] {'rows_0','rows_1','ro..., dimensions={0} | all-to-all | bytes 655360 | tf_op jit(solution)/shard_map/all_to_all | solution.py:370
  75.9 2.2 %step2.1 = (f32[128,128]{1,0:T(8,128)S(1)}, f32[128,128]{1,0:T(8,128)S(1)}, f32[8,128]{1,0:T(8,128)S(1)}) custom-call(bf16[53248,128]{1,0:T(8,128)(2,1)S(1)} %get-tuple-element.33.refs_0_, s32[208]{0:T(256)S(4)} %get-tuple-element.26.refs_2_.refs_1_, s32[208]{0:T(256)S(4)} %get-tuple-element.27.refs_3_.refs_2_, ...), custom_call_target="tpu_custom_call" | custom-call | tf_op jit(solution)/shard_map/step2/pallas_call | solution.py:442
  78.2 14.1 %all_to_all.29 = f32[128,1,128]{2,1,0:T(1,128)S(1)} all-to-all(f32[128,1,128]{2,1,0:T(1,128)S(1)} %bitcast.31), channel_id=1, replica_groups=mesh['rows_0'=4,'rows_1'=4,'rows_2'=4,'rows_3'=2] {'rows_0','rows_1','ro..., dimensions={0} | all-to-all | bytes 131072 | tf_op jit(solution)/shard_map/all_to_all | solution.py:370
  92.3 0.8 final.1
Async XLA Ops:
  23.1 15.6 %copy-start = (f32[208,128,128]{2,1,0:T(8,128)S(1)}, f32[208,128,128]{2,1,0:T(8,128)}, u32[]{:S(2)}) copy-start(f32[208,128,128]{2,1,0:T(8,128)} %refs_1_.1) | copy-start | bytes 40894468

commit v8 on v7

--- a/solution.py
+++ b/solution.py
@@ -17,7 +17,7 @@
 EPSILON = 1e-06
 
 TOTALS = 4
-TURNED = 4
+TURNED = 3
 COVER = 20_000_000_000
 MIB = 1 << 20
 

time: 93.4 us -> 93.3 us (level)
  no operation moved by 1% of the time
where the time goes in v8:
time: 93.3 us; the launch traced here: 93 us
  blocking collectives  82.1 us (88%)
  Pallas kernels  9.61 us (10%)
  between operations  1.31 us (1%)
    all_to_all x5, blocking collectives, exchange(): lax.all_to_all(outgoing.reshape(size, 1, 128), ROWS, split_axis=0, concat...  82.1 us
    pallas_call x3, Pallas kernels, on_device(): pl.pallas_call(functools.partial(step_kernel, step, last), out_shape=shap...  7.62 us

profile of v8, /device:TPU:1, one launch (start us, length us, event | category | flops | bytes accessed | tf_op | source)
XLA Modules:
  0.0 93.0 jit_solution(6194009090661373648)
XLA Ops:
  1.3 1.0 %begin.1 = (f32[128,128]{1,0:T(8,128)S(1)}, f32[128,128]{1,0:T(8,128)S(1)}, s32[208]{0:T(256)S(4)}, s32[208]{0:T(256)S(4)}, s32[1]{0:T(128)S(4)}) custom-call(s32[1]{0:T(128)S(6)} %copy.13.refs_0_, s32[1,128]{1,0:T(1,128)} %bitcast.35, f32[64,128]{1,0:T(8,128)} %bitcast.34, s32[208]{0:T(256)} %refs_3_.1, s32[208]{0:T(256)} %refs_4_.1), custom_call_target="tpu_custom_call" | custom-call | tf_op jit(solution)/shard_map/begin/pallas_call | solution.py:385
  2.2 20.8 %all_to_all.25 = f32[128,1,128]{2,1,0:T(1,128)S(1)} all-to-all(f32[128,1,128]{2,1,0:T(1,128)S(1)} %bitcast.32), channel_id=1, replica_groups=mesh['rows_0'=4,'rows_1'=4,'rows_2'=4,'rows_3'=2] {'rows_0','rows_1','ro..., dimensions={0} | all-to-all | bytes 131072 | tf_op jit(solution)/shard_map/all_to_all | solution.py:370
  23.1 0.0 copy-start
  23.1 0.2 first.1
  23.3 15.3 %all_to_all.26 = f32[512,1,128]{2,1,0:T(1,128)S(1)} all-to-all(f32[512,1,128]{2,1,0:T(1,128)S(1)} %bitcast.29), channel_id=1, replica_groups=mesh['rows_0'=4,'rows_1'=4,'rows_2'=4,'rows_3'=2] {'rows_0','rows_1','ro..., dimensions={0} | all-to-all | bytes 524288 | tf_op jit(solution)/shard_map/all_to_all | solution.py:370
  38.6 0.0 copy-done
  38.6 3.1 %step0.1 = (f32[128,128]{1,0:T(8,128)S(1)}, f32[640,128]{1,0:T(8,128)S(1)}, f32[656,128]{1,0:T(8,128)S(1)}, f32[128,128]{1,0:T(8,128)S(1)}, bf16[53248,128]{1,0:T(8,128)(2,1)S(1)}) custom-call(s32[1]{0:T(128)S(4)} %get-tuple-element.25.refs_0_, f32[208,128,128]{2,1,0:T(8,128)S(1)} %copy-done, s32[208]{0:T(256)S(4)} %get-tuple-element.26.refs_2_.refs_1_, ...), custom_call_target="tpu_custom_call" | custom-call | tf_op jit(solution)/shard_map/step0/pallas_call | solution.py:442
  41.8 15.8 %all_to_all.27 = f32[640,1,128]{2,1,0:T(1,128)S(1)} all-to-all(f32[640,1,128]{2,1,0:T(1,128)S(1)} %bitcast.27), channel_id=1, replica_groups=mesh['rows_0'=4,'rows_1'=4,'rows_2'=4,'rows_3'=2] {'rows_0','rows_1','ro..., dimensions={0} | all-to-all | bytes 655360 | tf_op jit(solution)/shard_map/all_to_all | solution.py:370
  57.6 2.2 %step1.1 = (f32[128,128]{1,0:T(8,128)S(1)}, f32[640,128]{1,0:T(8,128)S(1)}, f32[8,128]{1,0:T(8,128)S(1)}, f32[656,128]{1,0:T(8,128)S(1)}, f32[128,128]{1,0:T(8,128)S(1)}) custom-call(bf16[53248,128]{1,0:T(8,128)(2,1)S(1)} %get-tuple-element.33.refs_0_, s32[208]{0:T(256)S(4)} %get-tuple-element.26.refs_2_.refs_1_, s32[208]{0:T(256)S(4)} %get-tuple-element.27.refs_3_.refs_2_, ...), custom_call_target="tpu_custom_call" | custom-call | tf_op jit(solution)/shard_map/step1/pallas_call | solution.py:442
  59.8 16.0 %all_to_all.28 = f32[640,1,128]{2,1,0:T(1,128)S(1)} all-to-all(f32[640,1,128]{2,1,0:T(1,128)S(1)} %bitcast.28), channel_id=1, replica_groups=mesh['rows_0'=4,'rows_1'=4,'rows_2'=4,'rows_3'=2] {'rows_0','rows_1','ro..., dimensions={0} | all-to-all | bytes 655360 | tf_op jit(solution)/shard_map/all_to_all | solution.py:370
  75.8 2.2 %step2.1 = (f32[128,128]{1,0:T(8,128)S(1)}, f32[128,128]{1,0:T(8,128)S(1)}, f32[8,128]{1,0:T(8,128)S(1)}) custom-call(bf16[53248,128]{1,0:T(8,128)(2,1)S(1)} %get-tuple-element.33.refs_0_, s32[208]{0:T(256)S(4)} %get-tuple-element.26.refs_2_.refs_1_, s32[208]{0:T(256)S(4)} %get-tuple-element.27.refs_3_.refs_2_, ...), custom_call_target="tpu_custom_call" | custom-call | tf_op jit(solution)/shard_map/step2/pallas_call | solution.py:442
  78.1 14.1 %all_to_all.29 = f32[128,1,128]{2,1,0:T(1,128)S(1)} all-to-all(f32[128,1,128]{2,1,0:T(1,128)S(1)} %bitcast.31), channel_id=1, replica_groups=mesh['rows_0'=4,'rows_1'=4,'rows_2'=4,'rows_3'=2] {'rows_0','rows_1','ro..., dimensions={0} | all-to-all | bytes 131072 | tf_op jit(solution)/shard_map/all_to_all | solution.py:370
  92.2 0.8 final.1
Async XLA Ops:
  23.1 15.6 %copy-start = (f32[208,128,128]{2,1,0:T(8,128)S(1)}, f32[208,128,128]{2,1,0:T(8,128)}, u32[]{:S(2)}) copy-start(f32[208,128,128]{2,1,0:T(8,128)} %refs_1_.1) | copy-start | bytes 40894468
